TPU v7x, 256 devices: a whole 4x4x8 slice. The times are simulated.
256 devices in a mesh: ka: 32 (over z_hi, y, core), freq: 8 (over z_lo, x).
Axes of the slice: x: 4, y: 4, z: 8 (z_hi: 4, z_lo: 2; z = z_hi * 2 + z_lo), core: 2. Of those that a mesh axis runs over, the one named last changes fastest.
Arguments:
- energy: float32 [32, 128], P('ka'), may hold values from -2.4 to 2.4, as said below
- projector: float32 [32, 2, 128, 40], P('ka'), may hold values from -0.25 to 0.25
- self_energy: float32 [128, 2, 40, 40], P('freq'), may hold values from -0.5 to 0.5
- multiplicity: int32 [32], P('ka'), may hold values from 1 to 5
- orbitals: float32 [32, 2, 128, 32, 1024], P('ka', None, None, None, 'freq'), may hold values from -12 to 12
- owner: int32 [32], replicated, may hold values from 0 to 31, each once
- rotation: float32 [40, 40], replicated, may hold values from -1 to 1
Outputs:
- local_green: float32 [128, 2, 40, 40], P('freq')
- slab_charge: float32 [32, 1024], P('ka', 'freq')
Inputs may be any that keep to these rules, and one draw needn't show every extreme that they name: Every band energy has a magnitude between 1.6 and 2.4. `owner`: each ka index owns exactly one slab.
All inputs are finite; a program needn't handle non-finite values.
Results may differ from a plain program's by a relative error of at most 0.0001.
Values sent between devices are 32-bit elements; how exact they have to be, the bound alone decides.
No kernel may reach another device: no remote copies, remote signals or barrier semaphores. Data moves between devices by JAX's collectives and lax.ppermute only.
A program may use at most 64 MiB of HBM per device.

v0:
```python
import math

import jax
import jax.numpy as jnp
from jax import lax
from jax.experimental import pallas as pl
from jax.experimental.pallas import tpu as pltpu
from jax.sharding import PartitionSpec as P

F32 = jnp.float32
BF16 = jnp.bfloat16
LANES = 128
WIDE = 3
PIECE = 16


def low(x):
    return x - x.astype(BF16).astype(F32)


def mm(a, b):
    return jnp.dot(a, b, preferred_element_type=F32)


def mm3(a, b, b_low):
    rows = a.shape[0]
    both = mm(jnp.concatenate([a, low(a)], axis=0), b)
    return both[:rows] + both[rows:] + mm(a, b_low)


def blocks(wide, masks):
    n = wide.shape[0]
    rows = [jnp.where(m, wide, 0.0) for m in masks]
    rows.append(jnp.zeros((LANES - WIDE * n, LANES), F32))
    return jnp.concatenate(rows, axis=0)


def block_weights(wide, masks):
    def form(w):
        re = blocks(w[:, :LANES], masks)
        im = blocks(w[:, LANES:], masks)
        return jnp.concatenate(
            [jnp.concatenate([re, im], axis=1), jnp.concatenate([-im, re], axis=1)], axis=0
        )

    return form(wide), form(low(wide))


def green_kernel(pole_total, orbital_count, pole_stride, thermal_level):
    groups = -(-pole_total // WIDE)
    n = orbital_count

    def kernel(mult_ref, energy_ref, proj_ref, self_ref, rot_ref, dens_ref, rows_ref, flat_ref):
        weight = mult_ref[0].astype(F32)
        shift = lax.axis_index("freq")
        lane = lax.broadcasted_iota(jnp.int32, (n, LANES), 1)
        masks = [(lane >= n * j) & (lane < n * (j + 1)) for j in range(WIDE)]
        energy = energy_ref[...]
        pt = (proj_ref[0, 0], proj_ref[0, 1])
        step = math.pi * thermal_level

        def spread(x):
            tail = jnp.zeros((LANES - WIDE * n, LANES), F32)
            return jnp.concatenate([x] * WIDE + [tail], axis=0).T

        p3 = (spread(pt[0]), spread(pt[1]))
        energy_col = jnp.broadcast_to(energy, (LANES, LANES)).T
        rot = rot_ref[...]
        pt_both = jnp.concatenate([pt[0], pt[1]], axis=1)
        rot_t = rot.T
        turned = mm3(rot_t, pt_both, low(pt_both))
        left = jnp.concatenate([pt_both, turned], axis=0)
        rot_wide = jnp.concatenate([rot] * WIDE + [jnp.zeros((n, LANES - WIDE * n), F32)], axis=1)
        zero = jnp.zeros((LANES, LANES), F32)

        def rot_form(w):
            b = blocks(w, masks)
            return jnp.concatenate(
                [jnp.concatenate([b, zero], axis=1), jnp.concatenate([zero, b], axis=1)], axis=0
            )

        lane_row = lax.broadcasted_iota(jnp.int32, (1, LANES), 1)
        block_of = jnp.where(lane_row >= 2 * n, 2, jnp.where(lane_row >= n, 1, 0))

        gp = []
        for g in range(groups):
            slot = block_of + WIDE * g
            pole = (2 * (slot * pole_stride + shift) + 1).astype(F32) * step
            inv = 1.0 / (pole * pole + energy_col * energy_col)
            br = -energy_col * inv
            bi = -pole * inv
            gp.append((br * p3[0] - bi * p3[1], br * p3[1] + bi * p3[0]))

        big = []
        for g in range(groups):
            xr, xi = gp[g]

            def form(r, i):
                return jnp.concatenate(
                    [jnp.concatenate([r, i], axis=1), jnp.concatenate([i, -r], axis=1)], axis=0
                )

            big.append(mm3(left, form(xr, xi), form(low(xr), low(xi))))
        small = [b[:n] for b in big]
        stacked = jnp.concatenate(big, axis=0)
        right = mm3(stacked, rot_form(rot_wide), rot_form(low(rot_wide)))
        small_right = [right[2 * n * g : 2 * n * g + n] for g in range(groups)]
        both_right = [right[2 * n * g + n : 2 * n * (g + 1)] for g in range(groups)]

        sig = []
        pad = jnp.zeros((n, LANES - WIDE * n), F32)
        none = jnp.zeros((n, n), F32)
        for g in range(groups):
            halves = []
            for c in range(2):
                parts = []
                for j in range(WIDE):
                    q = WIDE * g + j
                    parts.append(self_ref[q, c] if q < pole_total else none)
                halves.append(jnp.concatenate(parts + [pad], axis=1))
            sig.append(jnp.concatenate(halves, axis=1))

        first = [mm3(big[g], *block_weights(sig[g], masks)) for g in range(groups)]
        a1 = [f[:n] for f in first]
        a1_left = [f[n:] for f in first]
        a2 = [mm3(a1[g], *block_weights(a1[g], masks)) for g in range(groups)]
        total = []
        for g in range(groups):
            w = block_weights(a2[g], masks)
            a34 = mm3(jnp.concatenate([a1[g], a2[g]], axis=0), *w)
            a34 = a34[:n] + a34[n:]
            total.append(a1[g] + a2[g] + a34 + mm3(a34, *w))
        last = [
            mm3(jnp.concatenate([sig[g], a1_left[g]], axis=0), *block_weights(total[g], masks))
            for g in range(groups)
        ]
        dress = [sig[g] + last[g][:n] for g in range(groups)]

        acc = None
        for g in range(groups):
            xr, xi = gp[g]
            w = mm3(jnp.concatenate([xr, xi], axis=1), *block_weights(dress[g], masks))
            res, ims = [], []
            for j in range(WIDE):
                q = WIDE * g + j
                pole = (2 * (q * pole_stride + shift) + 1).astype(F32) * step
                inv = 1.0 / (pole * pole + energy * energy)
                br = -energy * inv
                bi = -pole * inv
                res.append(pt[0] * br + pt[1] * bi)
                ims.append(pt[0] * bi - pt[1] * br)
            tail = jnp.zeros((LANES - WIDE * n, LANES), F32)
            re = jnp.concatenate(res + [tail], axis=0)
            im = jnp.concatenate(ims + [tail], axis=0)

            def form(r, i):
                return jnp.concatenate(
                    [jnp.concatenate([r, i], axis=1), jnp.concatenate([-i, r], axis=1)], axis=0
                )

            part = mm3(w, form(re, im), form(low(re), low(im)))
            acc = part if acc is None else acc + part
        er = acc[:, :LANES]
        ei = acc[:, LANES:]
        row = lax.broadcasted_iota(jnp.int32, (LANES, LANES), 0)
        col = lax.broadcasted_iota(jnp.int32, (LANES, LANES), 1)
        scale = weight * thermal_level
        dens_ref[...] = scale * jnp.where(row <= col, er + er.T, ei - ei.T)

        for g in range(groups):
            out = both_right[g] + mm3(
                a1_left[g] + last[g][n:], *block_weights(small_right[g], masks)
            )
            out = weight * out
            flat_ref[2 * n * g : 2 * n * g + n, :] = out[:, :LANES]
            flat_ref[2 * n * g + n : 2 * n * (g + 1), :] = out[:, LANES:]
        per = PIECE - 1
        for d in range(rows_ref.shape[0]):
            rows_ref[d, 0:per, :] = flat_ref[per * d : per * (d + 1), :]
            rows_ref[d, per:PIECE, :] = jnp.broadcast_to(weight, (1, LANES))

    return kernel


def split_kernel(orb_ref, high_ref, other_ref):
    bands = 2 * orb_ref.shape[2]
    slabs = orb_ref.shape[3]
    flat = orb_ref.reshape(bands * slabs, LANES)
    for s in range(slabs):
        x = flat[pl.ds(s, bands, stride=slabs), :]
        h = x.astype(BF16)
        high_ref[s] = h
        other_ref[s] = 2.0 * x - h.astype(F32)


def charge_kernel(owner_ref, dens_ref, local_ref, high_ref, other_ref, out_ref):
    packed = jnp.sum(dens_ref[...], axis=0)
    packed_t = packed.T
    row = lax.broadcasted_iota(jnp.int32, packed.shape, 0)
    col = lax.broadcasted_iota(jnp.int32, packed.shape, 1)
    re = jnp.where(row <= col, packed, packed_t)
    im = jnp.where(row > col, packed, jnp.where(row < col, -packed_t, 0.0))
    full = jnp.concatenate(
        [jnp.concatenate([re, -im], axis=1), jnp.concatenate([im, re], axis=1)], axis=0
    )
    high = full.astype(BF16)
    rest = (full - high.astype(F32)).astype(BF16)
    sums = jnp.sum(local_ref[...], axis=0)
    inverse = 1.0 / sums[PIECE - 1 : PIECE, :]
    sums = sums * inverse
    pieces = out_ref.shape[0]
    for d in range(pieces):
        out_ref[d] = sums
    slabs = high_ref.shape[0]
    for s in range(0, slabs, 2):
        cols = jnp.concatenate([high_ref[s], high_ref[s + 1]], axis=1)
        prod = mm(high, cols) + mm(rest, cols)
        for t in range(2):
            rho = jnp.sum(
                other_ref[s + t] * prod[:, LANES * t : LANES * (t + 1)], axis=0, keepdims=True
            )
            out_ref[owner_ref[s + t], PIECE - 1 : PIECE, :] = rho * inverse


def unpack_kernel(pole_total, orbital_count):
    n = orbital_count

    def kernel(in_ref, green_ref, charge_ref, flat_ref):
        per = PIECE - 1
        total = None
        for d in range(in_ref.shape[0]):
            flat_ref[per * d : per * (d + 1), :] = in_ref[d, 0:per, :]
            own = in_ref[d, per:PIECE, :]
            total = own if total is None else total + own
        charge_ref[...] = total
        for q in range(pole_total):
            g, j = divmod(q, WIDE)
            for c in range(2):
                base = n * (2 * g + c)
                green_ref[q, c] = flat_ref[base : base + n, n * j : n * (j + 1)]

    return kernel


def whole(memory=None):
    return pl.BlockSpec(memory_space=memory or pltpu.VMEM)


def local(energy, projector, self_energy, multiplicity, orbitals, owner, rotation):
    pole_total = self_energy.shape[0]
    n = self_energy.shape[2]
    slabs = orbitals.shape[3]
    peers = lax.axis_size("ka")
    poles = lax.axis_size("freq")
    bands = projector.shape[2]
    thermal_level = 0.25 / (pole_total * poles)
    groups = -(-pole_total // WIDE)
    flat_rows = 2 * n * groups
    assert flat_rows == (PIECE - 1) * peers and bands == LANES

    dens, rows = pl.pallas_call(
        green_kernel(pole_total, n, poles, thermal_level),
        out_shape=(
            jax.ShapeDtypeStruct((bands, bands), F32),
            jax.ShapeDtypeStruct((peers, PIECE, LANES), F32),
        ),
        in_specs=[whole(pltpu.SMEM), whole(), whole(), whole(), whole()],
        out_specs=(whole(), whole()),
        scratch_shapes=[pltpu.VMEM((flat_rows, LANES), F32)],
        name="green",
    )(multiplicity, energy, jnp.swapaxes(projector, 2, 3), self_energy, rotation)

    rows_in = lax.all_to_all(rows, "ka", 0, 0, tiled=True)
    dens_in = lax.all_to_all(
        jnp.broadcast_to(dens[None], (poles, *dens.shape)), "freq", 0, 0, tiled=True
    )

    step = 8
    high, other = pl.pallas_call(
        split_kernel,
        grid=(slabs // step,),
        in_specs=[pl.BlockSpec((1, 2, bands, step, LANES), lambda i: (0, 0, 0, i, 0))],
        out_specs=(
            pl.BlockSpec((step, 2 * bands, LANES), lambda i: (i, 0, 0)),
            pl.BlockSpec((step, 2 * bands, LANES), lambda i: (i, 0, 0)),
        ),
        out_shape=(
            jax.ShapeDtypeStruct((slabs, 2 * bands, LANES), BF16),
            jax.ShapeDtypeStruct((slabs, 2 * bands, LANES), F32),
        ),
        name="split",
    )(orbitals)

    sends = pl.pallas_call(
        charge_kernel,
        out_shape=jax.ShapeDtypeStruct((peers, PIECE, LANES), F32),
        in_specs=[whole(pltpu.SMEM), whole(), whole(), whole(), whole()],
        out_specs=whole(),
        name="charge",
    )(owner, dens_in, rows_in, high, other)
    back = lax.all_to_all(sends, "ka", 0, 0, tiled=True)

    local_green, slab = pl.pallas_call(
        unpack_kernel(pole_total, n),
        out_shape=(
            jax.ShapeDtypeStruct((pole_total, 2, n, n), F32),
            jax.ShapeDtypeStruct((1, LANES), F32),
        ),
        in_specs=[whole()],
        out_specs=(whole(), whole()),
        scratch_shapes=[pltpu.VMEM((flat_rows, LANES), F32)],
        name="unpack",
    )(back)
    return (local_green, slab)


def solution(mesh):
    in_specs = (
        P("ka", None),
        P("ka", None, None, None),
        P("freq", None, None, None),
        P("ka"),
        P("ka", None, None, None, "freq"),
        P(),
        P(),
    )
    out_specs = (P("freq", None, None, None), P("ka", "freq"))
    return jax.shard_map(local, mesh=mesh, in_specs=in_specs, out_specs=out_specs, check_vma=False)
```

profile of v0, /device:TPU:1, one launch (start us, length us, event | category | flops | bytes accessed | tf_op | source)
XLA Modules:
  0.0 74.7 jit_solution(14558819539407632693)
XLA Ops:
  1.3 5.1 %green.1 = (f32[128,128]{1,0:T(8,128)}, f32[32,16,128]{2,1,0:T(8,128)}) custom-call(s32[1]{0:T(128)S(6)} %copy.9.mult_ref, f32[1,128]{1,0:T(1,128)} %energy_ref.1, f32[1,2,40,128]{3,2,1,0:T(8,128)} %bitcast.1, f32[16,2,40,40]{3,2,1,0:T(8,128)} %self_ref.1, f32[40,40]{1,0:T(8,128)} %rot_ref.1), custom_call_target="tpu_custom_call" | custom-call | tf_op jit(solution)/shard_map/green/pallas_call | solution.py:261
  6.4 26.2 %all_to_all.15.local_ref = f32[32,16,128]{2,1,0:T(8,128)} all-to-all(f32[32,16,128]{2,1,0:T(8,128)} %get-tuple-element.7), channel_id=1, replica_groups=mesh['ka'=32,'freq'=8] {'ka'}, dimensions={0} | all-to-all | bytes 524288 | tf_op jit(solution)/shard_map/all_to_all | solution.py:273
  32.6 1.7 %broadcast_in_dim.2 = f32[8,128,128]{2,1,0:T(8,128)} broadcast(f32[128,128]{1,0:T(8,128)} %get-tuple-element.6), dimensions={1,2} | broadcast | bytes 589824 | tf_op jit(solution)/shard_map/broadcast_in_dim | solution.py:275
  34.3 4.3 %all-to-all-start = ((f32[8,128,128]{2,1,0:T(8,128)}), f32[8,128,128]{2,1,0:T(8,128)S(1)}, u32[]{:S(2)}, u32[]{:S(2)}) async-start(f32[8,128,128]{2,1,0:T(8,128)} %broadcast_in_dim.2), calls=%async_computation | async-start | bytes 1048576 | tf_op jit(solution)/shard_map/all_to_all | solution.py:274
  38.6 5.7 %split.1 = (bf16[32,256,128]{2,1,0:T(8,128)(2,1)}, f32[32,256,128]{2,1,0:T(8,128)}) custom-call(f32[1,2,128,32,128]{4,3,2,1,0:T(8,128)} %orb_ref.1), custom_call_target="tpu_custom_call" | custom-call | tf_op jit(solution)/shard_map/split/pallas_call | solution.py:279
  44.3 2.9 %all-to-all-done.dens_ref = f32[8,128,128]{2,1,0:T(8,128)S(1)} async-done(((f32[8,128,128]{2,1,0:T(8,128)}), f32[8,128,128]{2,1,0:T(8,128)S(1)}, u32[]{:S(2)}, u32[]{:S(2)}) %all-to-all-start) | async-done | bytes 524320 | tf_op jit(solution)/shard_map/all_to_all | solution.py:274
  47.1 0.0 copy-start
  47.1 0.8 %copy-done = f32[8,128,128]{2,1,0:T(8,128)} copy-done((f32[8,128,128]{2,1,0:T(8,128)}, f32[8,128,128]{2,1,0:T(8,128)S(1)}, u32[]{:S(2)}) %copy-start) | copy-done | bytes 524312
  47.9 5.1 %charge.1 = f32[32,16,128]{2,1,0:T(8,128)} custom-call(s32[32]{0:T(128)} %owner_ref.1, f32[8,128,128]{2,1,0:T(8,128)} %copy-done, f32[32,16,128]{2,1,0:T(8,128)} %all_to_all.15.local_ref, bf16[32,256,128]{2,1,0:T(8,128)(2,1)} %get-tuple-element.8.high_ref, f32[32,256,128]{2,1,0:T(8,128)} %get-tuple-element.9.other_ref), custom_call_target="tpu_custom_call" | custom-call | tf_op jit(solution)/shard_map/charge/pallas_call | solution.py:294
  53.0 19.7 %all_to_all.16.in_ref = f32[32,16,128]{2,1,0:T(8,128)} all-to-all(f32[32,16,128]{2,1,0:T(8,128)} %charge.1), channel_id=1, replica_groups=mesh['ka'=32,'freq'=8] {'ka'}, dimensions={0} | all-to-all | bytes 524288 | tf_op jit(solution)/shard_map/all_to_all | solution.py:301
  72.7 2.0 %unpack.1 = (f32[16,2,40,40]{3,2,1,0:T(8,128)}, f32[1,128]{1,0:T(1,128)}) custom-call(f32[32,16,128]{2,1,0:T(8,128)} %all_to_all.16.in_ref), custom_call_target="tpu_custom_call" | custom-call | tf_op jit(solution)/shard_map/unpack/pallas_call | solution.py:303
Async XLA Ops:
  34.3 12.8 %all-to-all-start = ((f32[8,128,128]{2,1,0:T(8,128)}), f32[8,128,128]{2,1,0:T(8,128)S(1)}, u32[]{:S(2)}, u32[]{:S(2)}) async-start(f32[8,128,128]{2,1,0:T(8,128)} %broadcast_in_dim.2), calls=%async_computation | async-start | bytes 1048576 | tf_op jit(solution)/shard_map/all_to_all | solution.py:274
  47.1 0.8 %copy-start = (f32[8,128,128]{2,1,0:T(8,128)}, f32[8,128,128]{2,1,0:T(8,128)S(1)}, u32[]{:S(2)}) copy-start(f32[8,128,128]{2,1,0:T(8,128)S(1)} %all-to-all-done.dens_ref) | copy-start | bytes 1572868
where the time goes:
time: 75.2 us; the launch traced here: 74.7 us
  blocking collectives  45.9 us (61%)
  Pallas kernels  17.9 us (24%)
  starting transfers between devices  4.28 us (6%)
  waiting for transfers between devices  2.87 us (4%)
  local copies, waits for them, and re-layouts  2.46 us (3%)
  between operations  1.28 us (2%)
    all_to_all x1, blocking collectives, local(): rows_in = lax.all_to_all(rows, 'ka', 0, 0, tiled=True)  26.2 us
    all_to_all x1, blocking collectives, local(): back = lax.all_to_all(sends, 'ka', 0, 0, tiled=True)  19.7 us
    pallas_call x1, Pallas kernels, local(): pl.pallas_call(split_kernel, grid=(slabs // step,), in_specs=[pl.BlockSpe...  5.67 us
    pallas_call x1, Pallas kernels, local(): pl.pallas_call(green_kernel(pole_total, n, poles, thermal_level), out_sha...  5.14 us
    pallas_call x1, Pallas kernels, local(): pl.pallas_call(charge_kernel, out_shape=jax.ShapeDtypeStruct((peers, PIEC...  5.14 us
    all_to_all x1, starting transfers between devices, local(): lax.all_to_all(jnp.broadcast_to(dens[None], (poles, *dens.shape)), 'freq'...  4.28 us
    all_to_all x1, waiting for transfers between devices, local(): lax.all_to_all(jnp.broadcast_to(dens[None], (poles, *dens.shape)), 'freq'...  2.87 us
    pallas_call x1, Pallas kernels, local(): pl.pallas_call(unpack_kernel(pole_total, n), out_shape=(jax.ShapeDtypeStr...  1.98 us
  transfers between devices with their start and end apart: 1, of which 1 were waited for; matrix products, arithmetic and copies ran while one was open for 0% of the time, Pallas kernels for 8%

commit v1 on v0

--- a/solution.py
+++ b/solution.py
@@ -6,6 +6,7 @@
 from jax.experimental import pallas as pl
 from jax.experimental.pallas import tpu as pltpu
 from jax.sharding import PartitionSpec as P
+
 
 F32 = jnp.float32
 BF16 = jnp.bfloat16
@@ -50,7 +51,11 @@
     groups = -(-pole_total // WIDE)
     n = orbital_count
 
-    def kernel(mult_ref, energy_ref, proj_ref, self_ref, rot_ref, dens_ref, rows_ref, flat_ref):
+    def kernel(
+        mult_ref, energy_ref, proj_ref, self_hbm, rot_ref, dens_ref, rows_ref, flat_ref, self_ref, sem
+    ):
+        fetch = pltpu.make_async_copy(self_hbm, self_ref, sem)
+        fetch.start()
         weight = mult_ref[0].astype(F32)
         shift = lax.axis_index("freq")
         lane = lax.broadcasted_iota(jnp.int32, (n, LANES), 1)
@@ -101,12 +106,12 @@
                 )
 
             big.append(mm3(left, form(xr, xi), form(low(xr), low(xi))))
-        small = [b[:n] for b in big]
         stacked = jnp.concatenate(big, axis=0)
         right = mm3(stacked, rot_form(rot_wide), rot_form(low(rot_wide)))
         small_right = [right[2 * n * g : 2 * n * g + n] for g in range(groups)]
         both_right = [right[2 * n * g + n : 2 * n * (g + 1)] for g in range(groups)]
 
+        fetch.wait()
         sig = []
         pad = jnp.zeros((n, LANES - WIDE * n), F32)
         none = jnp.zeros((n, n), F32)
@@ -186,15 +191,16 @@
     bands = 2 * orb_ref.shape[2]
     slabs = orb_ref.shape[3]
     flat = orb_ref.reshape(bands * slabs, LANES)
+    base = pl.program_id(0) * slabs
     for s in range(slabs):
         x = flat[pl.ds(s, bands, stride=slabs), :]
         h = x.astype(BF16)
-        high_ref[s] = h
-        other_ref[s] = 2.0 * x - h.astype(F32)
-
-
-def charge_kernel(owner_ref, dens_ref, local_ref, high_ref, other_ref, out_ref):
-    packed = jnp.sum(dens_ref[...], axis=0)
+        high_ref[base + s] = h
+        other_ref[base + s] = 2.0 * x - h.astype(F32)
+
+
+def slab_kernel(mine_ref, theirs_ref, high_ref, other_ref, out_ref):
+    packed = mine_ref[...] + theirs_ref[...]
     packed_t = packed.T
     row = lax.broadcasted_iota(jnp.int32, packed.shape, 0)
     col = lax.broadcasted_iota(jnp.int32, packed.shape, 1)
@@ -205,12 +211,6 @@
     )
     high = full.astype(BF16)
     rest = (full - high.astype(F32)).astype(BF16)
-    sums = jnp.sum(local_ref[...], axis=0)
-    inverse = 1.0 / sums[PIECE - 1 : PIECE, :]
-    sums = sums * inverse
-    pieces = out_ref.shape[0]
-    for d in range(pieces):
-        out_ref[d] = sums
     slabs = high_ref.shape[0]
     for s in range(0, slabs, 2):
         cols = jnp.concatenate([high_ref[s], high_ref[s + 1]], axis=1)
@@ -219,7 +219,17 @@
             rho = jnp.sum(
                 other_ref[s + t] * prod[:, LANES * t : LANES * (t + 1)], axis=0, keepdims=True
             )
-            out_ref[owner_ref[s + t], PIECE - 1 : PIECE, :] = rho * inverse
+            out_ref[s + t : s + t + 1, :] = rho
+
+
+def pack_kernel(owner_ref, local_ref, charge_ref, out_ref):
+    sums = jnp.sum(local_ref[...], axis=0)
+    inverse = 1.0 / sums[PIECE - 1 : PIECE, :]
+    sums = sums * inverse
+    for d in range(out_ref.shape[0]):
+        out_ref[d] = sums
+    for s in range(charge_ref.shape[0]):
+        out_ref[owner_ref[s], PIECE - 1 : PIECE, :] = charge_ref[s : s + 1, :] * inverse
 
 
 def unpack_kernel(pole_total, orbital_count):
@@ -246,6 +256,14 @@
     return pl.BlockSpec(memory_space=memory or pltpu.VMEM)
 
 
+def held(x):
+    return pltpu.with_memory_space_constraint(x, pltpu.VMEM)
+
+
+def far(x):
+    return pltpu.with_memory_space_constraint(x, pltpu.HBM)
+
+
 def local(energy, projector, self_energy, multiplicity, orbitals, owner, rotation):
     pole_total = self_energy.shape[0]
     n = self_energy.shape[2]
@@ -261,43 +279,65 @@
     dens, rows = pl.pallas_call(
         green_kernel(pole_total, n, poles, thermal_level),
         out_shape=(
-            jax.ShapeDtypeStruct((bands, bands), F32),
-            jax.ShapeDtypeStruct((peers, PIECE, LANES), F32),
+            pltpu.VMEM((bands, bands), F32),
+            pltpu.VMEM((peers, PIECE, LANES), F32),
         ),
-        in_specs=[whole(pltpu.SMEM), whole(), whole(), whole(), whole()],
+        in_specs=[whole(pltpu.SMEM), whole(), whole(), whole(pl.ANY), whole()],
         out_specs=(whole(), whole()),
-        scratch_shapes=[pltpu.VMEM((flat_rows, LANES), F32)],
+        scratch_shapes=[
+            pltpu.VMEM((flat_rows, LANES), F32),
+            pltpu.VMEM(self_energy.shape, F32),
+            pltpu.SemaphoreType.DMA,
+        ],
+        compiler_params=pltpu.CompilerParams(vmem_limit_bytes=20 << 20),
         name="green",
-    )(multiplicity, energy, jnp.swapaxes(projector, 2, 3), self_energy, rotation)
-
+    )(
+        multiplicity,
+        far(energy),
+        far(jnp.swapaxes(projector, 2, 3)),
+        far(self_energy),
+        far(rotation),
+    )
+
+    def swapped(x, flip):
+        return lax.ppermute(x, "freq", [(i, i ^ flip) for i in range(poles)])
+
+    theirs = swapped(dens, 4)
     rows_in = lax.all_to_all(rows, "ka", 0, 0, tiled=True)
-    dens_in = lax.all_to_all(
-        jnp.broadcast_to(dens[None], (poles, *dens.shape)), "freq", 0, 0, tiled=True
-    )
+    dens = dens + theirs
+    dens = dens + swapped(dens, 1)
+    theirs = swapped(dens, 3)
 
     step = 8
     high, other = pl.pallas_call(
         split_kernel,
         grid=(slabs // step,),
         in_specs=[pl.BlockSpec((1, 2, bands, step, LANES), lambda i: (0, 0, 0, i, 0))],
-        out_specs=(
-            pl.BlockSpec((step, 2 * bands, LANES), lambda i: (i, 0, 0)),
-            pl.BlockSpec((step, 2 * bands, LANES), lambda i: (i, 0, 0)),
+        out_specs=(whole(), whole()),
+        out_shape=(
+            pltpu.VMEM((slabs, 2 * bands, LANES), BF16),
+            pltpu.VMEM((slabs, 2 * bands, LANES), F32),
         ),
-        out_shape=(
-            jax.ShapeDtypeStruct((slabs, 2 * bands, LANES), BF16),
-            jax.ShapeDtypeStruct((slabs, 2 * bands, LANES), F32),
-        ),
+        compiler_params=pltpu.CompilerParams(vmem_limit_bytes=8 << 20),
         name="split",
-    )(orbitals)
-
+    )(far(orbitals))
+
+    rho = pl.pallas_call(
+        slab_kernel,
+        out_shape=pltpu.VMEM((slabs, LANES), F32),
+        in_specs=[whole()] * 4,
+        out_specs=whole(),
+        compiler_params=pltpu.CompilerParams(vmem_limit_bytes=8 << 20),
+        name="slab",
+    )(held(dens), held(theirs), held(high), held(other))
     sends = pl.pallas_call(
-        charge_kernel,
-        out_shape=jax.ShapeDtypeStruct((peers, PIECE, LANES), F32),
-        in_specs=[whole(pltpu.SMEM), whole(), whole(), whole(), whole()],
+        pack_kernel,
+        out_shape=pltpu.VMEM((peers, PIECE, LANES), F32),
+        in_specs=[whole(pltpu.SMEM), whole(), whole()],
         out_specs=whole(),
-        name="charge",
-    )(owner, dens_in, rows_in, high, other)
+        compiler_params=pltpu.CompilerParams(vmem_limit_bytes=4 << 20),
+        name="pack",
+    )(owner, held(rows_in), held(rho))
     back = lax.all_to_all(sends, "ka", 0, 0, tiled=True)
 
     local_green, slab = pl.pallas_call(
@@ -309,8 +349,9 @@
         in_specs=[whole()],
         out_specs=(whole(), whole()),
         scratch_shapes=[pltpu.VMEM((flat_rows, LANES), F32)],
+        compiler_params=pltpu.CompilerParams(vmem_limit_bytes=6 << 20),
         name="unpack",
-    )(back)
+    )(held(back))
     return (local_green, slab)
 
 

time: 75.2 us -> 65 us (0.86)
  blocking collectives: 45.9 us -> 23.9 us
  starting transfers between devices: 4.28 us -> 17.4 us
  waiting for transfers between devices: 2.87 us -> 10.2 us
  Pallas kernels: 17.9 us -> 11.7 us
  local copies, waits for them, and re-layouts: 2.46 us -> 0.01 us
    all_to_all x1 -> x0, blocking collectives: 26.2 us -> none  [local(): rows_in = lax.all_to_all(rows, 'ka', 0, 0, tiled=True)]
    ppermute x0 -> x3, waiting for transfers between devices: none -> 10.2 us  [swapped(): return lax.ppermute(x, 'freq', [(i, i ^ flip) for i in range(poles)])]
    all_to_all x1, starting transfers between devices: 4.28 us -> 12.8 us  [local(): rows_in = lax.all_to_all(rows, 'ka', 0, 0, tiled=True)]
    ppermute x0 -> x3, starting transfers between devices: none -> 4.68 us  [swapped(): return lax.ppermute(x, 'freq', [(i, i ^ flip) for i in range(poles)])]
    all_to_all x1, blocking collectives: 19.7 us -> 23.9 us  [local(): back = lax.all_to_all(sends, 'ka', 0, 0, tiled=True)]
    pallas_call x1 -> x2, Pallas kernels: 5.14 us -> 1.92 us  [the longest x1 1.31 us: local(): pl.pallas_call(slab_kernel, out_shape=pltpu.VMEM((slabs, LANES), F32), in...]
    all_to_all x1, waiting for transfers between devices: 2.87 us -> 0.01 us  [local(): rows_in = lax.all_to_all(rows, 'ka', 0, 0, tiled=True)]
    pallas_call x1, Pallas kernels: 5.67 us -> 3.42 us  [local(): pl.pallas_call(split_kernel, grid=(slabs // step,), in_specs=[pl.BlockSpe...]
  transfers between devices with their start and end apart: 1 -> 4, of which waited for: 1 -> 2; matrix products, arithmetic and copies ran while one was open for 0% -> 0% of each run, Pallas kernels for 8% -> 7%
where the time goes in v1:
time: 65 us; the launch traced here: 64.6 us
  blocking collectives  23.9 us (37%)
  starting transfers between devices  17.4 us (27%)
  Pallas kernels  11.7 us (18%)
  waiting for transfers between devices  10.2 us (16%)
  between operations  1.36 us (2%)
    all_to_all x1, blocking collectives, local(): back = lax.all_to_all(sends, 'ka', 0, 0, tiled=True)  23.9 us
    all_to_all x1, starting transfers between devices, local(): rows_in = lax.all_to_all(rows, 'ka', 0, 0, tiled=True)  12.8 us
    ppermute x3, waiting for transfers between devices, swapped(): return lax.ppermute(x, 'freq', [(i, i ^ flip) for i in range(poles)])  10.2 us
    pallas_call x1, Pallas kernels, local(): pl.pallas_call(green_kernel(pole_total, n, poles, thermal_level), out_sha...  5.31 us
    ppermute x3, starting transfers between devices, swapped(): return lax.ppermute(x, 'freq', [(i, i ^ flip) for i in range(poles)])  4.68 us
    pallas_call x1, Pallas kernels, local(): pl.pallas_call(split_kernel, grid=(slabs // step,), in_specs=[pl.BlockSpe...  3.42 us
    pallas_call x1, Pallas kernels, local(): pl.pallas_call(slab_kernel, out_shape=pltpu.VMEM((slabs, LANES), F32), in...  1.31 us
  transfers between devices with their start and end apart: 4, of which 2 were waited for; matrix products, arithmetic and copies ran while one was open for 0% of the time, Pallas kernels for 7%

profile of v1, /device:TPU:1, one launch (start us, length us, event | category | flops | bytes accessed | tf_op | source)
XLA Modules:
  0.0 64.6 jit_solution(15103800598961960259)
XLA Ops:
  1.3 5.3 %green.1 = (f32[128,128]{1,0:T(8,128)S(1)}, f32[32,16,128]{2,1,0:T(8,128)}) custom-call(s32[1]{0:T(128)S(6)} %copy.9.mult_ref, f32[1,128]{1,0:T(1,128)} %energy_ref.1, f32[1,2,40,128]{3,2,1,0:T(8,128)} %bitcast.1, f32[16,2,40,40]{3,2,1,0:T(8,128)} %self_hbm.1, f32[40,40]{1,0:T(8,128)} %rot_ref.1), custom_call_target="tpu_custom_call" | custom-call | tf_op jit(solution)/shard_map/green/pallas_call | solution.py:279
  6.6 12.8 %all-to-all-start = ((f32[32,16,128]{2,1,0:T(8,128)}), f32[32,16,128]{2,1,0:T(8,128)S(1)}, u32[]{:S(2)}, u32[]{:S(2)}) async-start(f32[32,16,128]{2,1,0:T(8,128)} %get-tuple-element.6), calls=%async_computation | async-start | bytes 524288 | tf_op jit(solution)/shard_map/all_to_all | solution.py:306
  19.4 0.8 %collective-permute-start = (f32[128,128]{1,0:T(8,128)S(1)}, f32[128,128]{1,0:T(8,128)S(1)}, u32[]{:S(2)}, u32[]{:S(2)}) collective-permute-start(f32[128,128]{1,0:T(8,128)S(1)} %get-tuple-element.7), channel_id=1, source_target_pairs={{0,4},{1,5},{2,6},{3,7},{4,0},{5,1},{6,2},{7,3},{8,12},{9,13},{10,... | collective-permute-start | bytes 196616 | tf_op jit(solution)/shard_map/ppermute | solution.py:303
  20.2 8.0 %collective-permute-done = f32[128,128]{1,0:T(8,128)S(1)} collective-permute-done((f32[128,128]{1,0:T(8,128)S(1)}, f32[128,128]{1,0:T(8,128)S(1)}, u32[]{:S(2)}, u32[]{:S(2)}) %collective-permute-start) | collective-permute-done | bytes 65568 | tf_op jit(solution)/shard_map/ppermute | solution.py:303
  28.2 1.3 %collective-permute-start.1 = (f32[128,128]{1,0:T(8,128)S(1)}, f32[128,128]{1,0:T(8,128)S(1)}, u32[]{:S(2)}, u32[]{:S(2)}) collective-permute-start(f32[128,128]{1,0:T(8,128)S(1)} %add.6), channel_id=1, source_target_pairs={{0,1},{1,0},{2,3},{3,2},{4,5},{5,4},{6,7},{7,6},{8,9},{9,8},{10,11... | collective-permute-start | bytes 196616 | tf_op jit(solution)/shard_map/ppermute | solution.py:303
  29.5 2.2 %collective-permute-done.1 = f32[128,128]{1,0:T(8,128)S(1)} collective-permute-done((f32[128,128]{1,0:T(8,128)S(1)}, f32[128,128]{1,0:T(8,128)S(1)}, u32[]{:S(2)}, u32[]{:S(2)}) %collective-permute-start.1) | collective-permute-done | bytes 65568 | tf_op jit(solution)/shard_map/ppermute | solution.py:303
  31.7 2.6 %collective-permute-start.2 = (f32[128,128]{1,0:T(8,128)S(1)}, f32[128,128]{1,0:T(8,128)S(1)}, u32[]{:S(2)}, u32[]{:S(2)}) collective-permute-start(f32[128,128]{1,0:T(8,128)S(1)} %add.7.mine_ref), channel_id=1, source_target_pairs={{0,3},{1,2},{2,1},{3,0},{4,7},{5,6},{6,5},{7,4},{8,11},{9,10},{10,... | collective-permute-start | bytes 196616 | tf_op jit(solution)/shard_map/ppermute | solution.py:303
  34.3 3.4 %split.1 = (bf16[32,256,128]{2,1,0:T(8,128)(2,1)S(1)}, f32[32,256,128]{2,1,0:T(8,128)S(1)}) custom-call(f32[1,2,128,32,128]{4,3,2,1,0:T(8,128)} %orb_ref.1), custom_call_target="tpu_custom_call" | custom-call | tf_op jit(solution)/shard_map/split/pallas_call | solution.py:312
  37.7 0.0 copy-start
  37.7 0.0 collective-permute-done.2.theirs_ref
  37.8 1.3 %slab.1.charge_ref = f32[32,128]{1,0:T(8,128)S(1)} custom-call(f32[128,128]{1,0:T(8,128)S(1)} %add.7.mine_ref, f32[128,128]{1,0:T(8,128)S(1)} %collective-permute-done.2.theirs_ref, bf16[32,256,128]{2,1,0:T(8,128)(2,1)S(1)} %get-tuple-element.8.high_ref, f32[32,256,128]{2,1,0:T(8,128)S(1)} %get-tuple-element.9.other_ref), custom_call_target="tpu_custom_call" | custom-call | tf_op jit(solution)/shard_map/slab/pallas_call | solution.py:325
  39.1 0.0 all-to-all-done.local_ref
  39.1 0.0 copy-done
  39.1 0.6 pack.1
  39.7 23.9 %all_to_all.10.in_ref = f32[32,16,128]{2,1,0:T(8,128)S(1)} all-to-all(f32[32,16,128]{2,1,0:T(8,128)S(1)} %pack.1), channel_id=1, replica_groups=mesh['ka'=32,'freq'=8] {'ka'}, dimensions={0} | all-to-all | bytes 524288 | tf_op jit(solution)/shard_map/all_to_all | solution.py:341
  63.6 1.0 %unpack.1 = (f32[16,2,40,40]{3,2,1,0:T(8,128)}, f32[1,128]{1,0:T(1,128)}) custom-call(f32[32,16,128]{2,1,0:T(8,128)S(1)} %all_to_all.10.in_ref), custom_call_target="tpu_custom_call" | custom-call | tf_op jit(solution)/shard_map/unpack/pallas_call | solution.py:343
  (2 shorter events, 0.0 us)
Async XLA Ops:
  6.6 32.5 %all-to-all-start = ((f32[32,16,128]{2,1,0:T(8,128)}), f32[32,16,128]{2,1,0:T(8,128)S(1)}, u32[]{:S(2)}, u32[]{:S(2)}) async-start(f32[32,16,128]{2,1,0:T(8,128)} %get-tuple-element.6), calls=%async_computation | async-start | bytes 524288 | tf_op jit(solution)/shard_map/all_to_all | solution.py:306
  19.4 8.9 %collective-permute-start = (f32[128,128]{1,0:T(8,128)S(1)}, f32[128,128]{1,0:T(8,128)S(1)}, u32[]{:S(2)}, u32[]{:S(2)}) collective-permute-start(f32[128,128]{1,0:T(8,128)S(1)} %get-tuple-element.7), channel_id=1, source_target_pairs={{0,4},{1,5},{2,6},{3,7},{4,0},{5,1},{6,2},{7,3},{8,12},{9,13},{10,... | collective-permute-start | bytes 196616 | tf_op jit(solution)/shard_map/ppermute | solution.py:303
  28.2 3.5 %collective-permute-start.1 = (f32[128,128]{1,0:T(8,128)S(1)}, f32[128,128]{1,0:T(8,128)S(1)}, u32[]{:S(2)}, u32[]{:S(2)}) collective-permute-start(f32[128,128]{1,0:T(8,128)S(1)} %add.6), channel_id=1, source_target_pairs={{0,1},{1,0},{2,3},{3,2},{4,5},{5,4},{6,7},{7,6},{8,9},{9,8},{10,11... | collective-permute-start | bytes 196616 | tf_op jit(solution)/shard_map/ppermute | solution.py:303
  31.7 6.0 %collective-permute-start.2 = (f32[128,128]{1,0:T(8,128)S(1)}, f32[128,128]{1,0:T(8,128)S(1)}, u32[]{:S(2)}, u32[]{:S(2)}) collective-permute-start(f32[128,128]{1,0:T(8,128)S(1)} %add.7.mine_ref), channel_id=1, source_target_pairs={{0,3},{1,2},{2,1},{3,0},{4,7},{5,6},{6,5},{7,4},{8,11},{9,10},{10,... | collective-permute-start | bytes 196616 | tf_op jit(solution)/shard_map/ppermute | solution.py:303
  37.7 1.4 %copy-start = (s32[32]{0:T(128)S(1)}, s32[32]{0:T(128)}, u32[]{:S(2)}) copy-start(s32[32]{0:T(128)} %owner_ref.1) | copy-start | bytes 388

commit v2 on v1

--- a/solution.py
+++ b/solution.py
@@ -52,7 +52,18 @@
     n = orbital_count
 
     def kernel(
-        mult_ref, energy_ref, proj_ref, self_hbm, rot_ref, dens_ref, rows_ref, flat_ref, self_ref, sem
+        mult_ref,
+        energy_ref,
+        proj_ref,
+        self_hbm,
+        rot_ref,
+        dens_ref,
+        keep_ref,
+        give_ref,
+        flat_ref,
+        rows_ref,
+        self_ref,
+        sem,
     ):
         fetch = pltpu.make_async_copy(self_hbm, self_ref, sem)
         fetch.start()
@@ -183,6 +194,12 @@
         for d in range(rows_ref.shape[0]):
             rows_ref[d, 0:per, :] = flat_ref[per * d : per * (d + 1), :]
             rows_ref[d, per:PIECE, :] = jnp.broadcast_to(weight, (1, LANES))
+        me = lax.axis_index("ka")
+        half = keep_ref.shape[0]
+        for r in range(half):
+            d = ((r % 4) * 8 + (r // 4) * 2) ^ me
+            keep_ref[r] = rows_ref[d]
+            give_ref[r] = rows_ref[d ^ 1]
 
     return kernel
 
@@ -222,8 +239,8 @@
             out_ref[s + t : s + t + 1, :] = rho
 
 
-def pack_kernel(owner_ref, local_ref, charge_ref, out_ref):
-    sums = jnp.sum(local_ref[...], axis=0)
+def pack_kernel(owner_ref, a_ref, b_ref, c_ref, d_ref, charge_ref, out_ref):
+    sums = (a_ref[...] + b_ref[...]) + (c_ref[...] + d_ref[...])
     inverse = 1.0 / sums[PIECE - 1 : PIECE, :]
     sums = sums * inverse
     for d in range(out_ref.shape[0]):
@@ -276,16 +293,18 @@
     flat_rows = 2 * n * groups
     assert flat_rows == (PIECE - 1) * peers and bands == LANES
 
-    dens, rows = pl.pallas_call(
+    dens, keep, give = pl.pallas_call(
         green_kernel(pole_total, n, poles, thermal_level),
         out_shape=(
             pltpu.VMEM((bands, bands), F32),
-            pltpu.VMEM((peers, PIECE, LANES), F32),
+            pltpu.VMEM((peers // 2, PIECE, LANES), F32),
+            pltpu.VMEM((peers // 2, PIECE, LANES), F32),
         ),
         in_specs=[whole(pltpu.SMEM), whole(), whole(), whole(pl.ANY), whole()],
-        out_specs=(whole(), whole()),
+        out_specs=(whole(), whole(), whole()),
         scratch_shapes=[
             pltpu.VMEM((flat_rows, LANES), F32),
+            pltpu.VMEM((peers, PIECE, LANES), F32),
             pltpu.VMEM(self_energy.shape, F32),
             pltpu.SemaphoreType.DMA,
         ],
@@ -299,14 +318,19 @@
         far(rotation),
     )
 
-    def swapped(x, flip):
-        return lax.ppermute(x, "freq", [(i, i ^ flip) for i in range(poles)])
-
-    theirs = swapped(dens, 4)
-    rows_in = lax.all_to_all(rows, "ka", 0, 0, tiled=True)
-    dens = dens + theirs
-    dens = dens + swapped(dens, 1)
-    theirs = swapped(dens, 3)
+    def swapped(x, axis, flip):
+        return lax.ppermute(x, axis, [(i, i ^ flip) for i in range(lax.axis_size(axis))])
+
+    theirs = swapped(give, "ka", 1)
+    other_dens = swapped(dens, "freq", 4)
+    rows = (keep + theirs).reshape(4, 4, PIECE, LANES)
+    arrived = [swapped(rows[d], "ka", 2 * d) for d in range(1, 4)]
+    rows = rows[0] + sum(arrived)
+    dens = dens + other_dens
+    other_dens = swapped(dens, "freq", 1)
+    dens = dens + other_dens
+    parts = [rows[0]] + [swapped(rows[d], "ka", 8 * d) for d in range(1, 4)]
+    theirs = swapped(dens, "freq", 3)
 
     step = 8
     high, other = pl.pallas_call(
@@ -321,7 +345,6 @@
         compiler_params=pltpu.CompilerParams(vmem_limit_bytes=8 << 20),
         name="split",
     )(far(orbitals))
-
     rho = pl.pallas_call(
         slab_kernel,
         out_shape=pltpu.VMEM((slabs, LANES), F32),
@@ -333,11 +356,11 @@
     sends = pl.pallas_call(
         pack_kernel,
         out_shape=pltpu.VMEM((peers, PIECE, LANES), F32),
-        in_specs=[whole(pltpu.SMEM), whole(), whole()],
+        in_specs=[whole(pltpu.SMEM)] + [whole()] * 5,
         out_specs=whole(),
         compiler_params=pltpu.CompilerParams(vmem_limit_bytes=4 << 20),
         name="pack",
-    )(owner, held(rows_in), held(rho))
+    )(owner, *[held(x) for x in parts], held(rho))
     back = lax.all_to_all(sends, "ka", 0, 0, tiled=True)
 
     local_green, slab = pl.pallas_call(

time: 65 us -> 58.6 us (0.902)
  waiting for transfers between devices: 10.2 us -> 4.84 us
  Pallas kernels: 11.7 us -> 11 us
    all_to_all x1 -> x0, starting transfers between devices: 12.8 us -> none  [local(): rows_in = lax.all_to_all(rows, 'ka', 0, 0, tiled=True)]
    ppermute x3 -> x10, starting transfers between devices: 4.68 us -> 16.8 us  [swapped(): lax.ppermute(x, axis, [(i, i ^ flip) for i in range(lax.axis_size(axis))])]
    ppermute x3 -> x10, waiting for transfers between devices: 10.2 us -> 4.84 us  [swapped(): lax.ppermute(x, axis, [(i, i ^ flip) for i in range(lax.axis_size(axis))])]
    pallas_call x1, Pallas kernels: 5.31 us -> 4.63 us  [local(): pl.pallas_call(green_kernel(pole_total, n, poles, thermal_level), out_sha...]
  transfers between devices with their start and end apart: 4 -> 10, of which waited for: 2 -> 2; matrix products, arithmetic and copies ran while one was open for 0% -> 0% of each run, Pallas kernels for 7% -> 8%
where the time goes in v2:
time: 58.6 us; the launch traced here: 58.3 us
  blocking collectives  24.2 us (41%)
  starting transfers between devices  16.8 us (29%)
  Pallas kernels  11 us (19%)
  waiting for transfers between devices  4.84 us (8%)
  between operations  1.41 us (2%)
    all_to_all x1, blocking collectives, local(): back = lax.all_to_all(sends, 'ka', 0, 0, tiled=True)  24.2 us
    ppermute x10, starting transfers between devices, swapped(): lax.ppermute(x, axis, [(i, i ^ flip) for i in range(lax.axis_size(axis))])  16.8 us
    ppermute x10, waiting for transfers between devices, swapped(): lax.ppermute(x, axis, [(i, i ^ flip) for i in range(lax.axis_size(axis))])  4.84 us
    pallas_call x1, Pallas kernels, local(): pl.pallas_call(green_kernel(pole_total, n, poles, thermal_level), out_sha...  4.63 us
    pallas_call x1, Pallas kernels, local(): pl.pallas_call(split_kernel, grid=(slabs // step,), in_specs=[pl.BlockSpe...  3.42 us
    pallas_call x1, Pallas kernels, local(): pl.pallas_call(slab_kernel, out_shape=pltpu.VMEM((slabs, LANES), F32), in...  1.31 us
  transfers between devices with their start and end apart: 10, of which 2 were waited for; matrix products, arithmetic and copies ran while one was open for 0% of the time, Pallas kernels for 8%

profile of v2, /device:TPU:1, one launch (start us, length us, event | category | flops | bytes accessed | tf_op | source)
XLA Modules:
  0.0 58.3 jit_solution(6516921703214561522)
XLA Ops:
  1.3 4.6 %green.1 = (f32[128,128]{1,0:T(8,128)S(1)}, f32[16,16,128]{2,1,0:T(8,128)S(1)}, f32[16,16,128]{2,1,0:T(8,128)S(1)}) custom-call(s32[1]{0:T(128)S(6)} %copy.9.mult_ref, f32[1,128]{1,0:T(1,128)} %energy_ref.1, f32[1,2,40,128]{3,2,1,0:T(8,128)} %bitcast.9, f32[16,2,40,40]{3,2,1,0:T(8,128)} %self_hbm.1, f32[40,40]{1,0:T(8,128)} %rot_ref.1), custom_call_target="tpu_custom_call" | custom-call | tf_op jit(solution)/shard_map/green/pallas_call | solution.py:296
  5.9 3.3 %collective-permute-start = (f32[16,16,128]{2,1,0:T(8,128)S(1)}, f32[16,16,128]{2,1,0:T(8,128)S(1)}, u32[]{:S(2)}, u32[]{:S(2)}) collective-permute-start(f32[16,16,128]{2,1,0:T(8,128)S(1)} %get-tuple-element.8), channel_id=1, source_target_pairs={{0,8},{8,0},{16,24},{24,16},{32,40},{40,32},{48,56},{56,48},{64,72... | collective-permute-start | bytes 393224 | tf_op jit(solution)/shard_map/ppermute | solution.py:322
  9.2 0.0 collective-permute-start.7
  9.2 3.5 %collective-permute-done.7 = f32[128,128]{1,0:T(8,128)S(1)} collective-permute-done((f32[128,128]{1,0:T(8,128)S(1)}, f32[128,128]{1,0:T(8,128)S(1)}, u32[]{:S(2)}, u32[]{:S(2)}) %collective-permute-start.7) | collective-permute-done | bytes 65568 | tf_op jit(solution)/shard_map/ppermute | solution.py:322
  12.8 0.1 collective-permute-start.8
  12.9 0.0 collective-permute-done
  12.9 2.8 %collective-permute-start.2 = (f32[4,16,128]{2,1,0:T(8,128)S(1)}, f32[4,16,128]{2,1,0:T(8,128)S(1)}, u32[]{:S(2)}, u32[]{:S(2)}) collective-permute-start(f32[4,16,128]{2,1,0:T(8,128)S(1)} %get-tuple-element.12), channel_id=1, source_target_pairs={{0,32},{8,40},{16,48},{24,56},{32,0},{40,8},{48,16},{56,24},{64,96... | collective-permute-start | bytes 98312 | tf_op jit(solution)/shard_map/ppermute | solution.py:322
  15.8 0.8 %collective-permute-start.3 = (f32[4,16,128]{2,1,0:T(8,128)S(1)}, f32[4,16,128]{2,1,0:T(8,128)S(1)}, u32[]{:S(2)}, u32[]{:S(2)}) collective-permute-start(f32[4,16,128]{2,1,0:T(8,128)S(1)} %get-tuple-element.13), channel_id=1, source_target_pairs={{0,48},{8,56},{16,32},{24,40},{32,16},{40,24},{48,0},{56,8},{64,11... | collective-permute-start | bytes 98312 | tf_op jit(solution)/shard_map/ppermute | solution.py:322
  16.5 0.0 collective-permute-start.1
  16.5 0.0 collective-permute-done.8
  16.5 1.9 %collective-permute-start.9 = (f32[128,128]{1,0:T(8,128)S(1)}, f32[128,128]{1,0:T(8,128)S(1)}, u32[]{:S(2)}, u32[]{:S(2)}) collective-permute-start(f32[128,128]{1,0:T(8,128)S(1)} %add.23.mine_ref), channel_id=1, source_target_pairs={{0,3},{1,2},{2,1},{3,0},{4,7},{5,6},{6,5},{7,4},{8,11},{9,10},{10,... | collective-permute-start | bytes 196616 | tf_op jit(solution)/shard_map/ppermute | solution.py:322
  18.4 0.0 collective-permute-done.2
  18.4 1.3 %collective-permute-done.3 = f32[4,16,128]{2,1,0:T(8,128)S(1)} collective-permute-done((f32[4,16,128]{2,1,0:T(8,128)S(1)}, f32[4,16,128]{2,1,0:T(8,128)S(1)}, u32[]{:S(2)}, u32[]{:S(2)}) %collective-permute-start.3) | collective-permute-done | bytes 32800 | tf_op jit(solution)/shard_map/ppermute | solution.py:322
  19.7 0.0 collective-permute-done.1
  19.8 5.8 %collective-permute-start.6 = (f32[16,128]{1,0:T(8,128)S(1)}, f32[16,128]{1,0:T(8,128)S(1)}, u32[]{:S(2)}, u32[]{:S(2)}) collective-permute-start(f32[16,128]{1,0:T(8,128)S(1)} %get-tuple-element.15), channel_id=1, source_target_pairs={{0,192},{8,200},{16,208},{24,216},{32,224},{40,232},{48,240},{56,2... | collective-permute-start | bytes 24584 | tf_op jit(solution)/shard_map/ppermute | solution.py:322
  25.5 1.0 %collective-permute-start.5 = (f32[16,128]{1,0:T(8,128)S(1)}, f32[16,128]{1,0:T(8,128)S(1)}, u32[]{:S(2)}, u32[]{:S(2)}) collective-permute-start(f32[16,128]{1,0:T(8,128)S(1)} %get-tuple-element.16), channel_id=1, source_target_pairs={{0,128},{8,136},{16,144},{24,152},{32,160},{40,168},{48,176},{56,1... | collective-permute-start | bytes 24584 | tf_op jit(solution)/shard_map/ppermute | solution.py:322
  26.5 1.2 %collective-permute-start.4 = (f32[16,128]{1,0:T(8,128)S(1)}, f32[16,128]{1,0:T(8,128)S(1)}, u32[]{:S(2)}, u32[]{:S(2)}) collective-permute-start(f32[16,128]{1,0:T(8,128)S(1)} %get-tuple-element.17), channel_id=1, source_target_pairs={{0,64},{8,72},{16,80},{24,88},{32,96},{40,104},{48,112},{56,120},{... | collective-permute-start | bytes 24584 | tf_op jit(solution)/shard_map/ppermute | solution.py:322
  27.7 3.4 %split.1 = (bf16[32,256,128]{2,1,0:T(8,128)(2,1)S(1)}, f32[32,256,128]{2,1,0:T(8,128)S(1)}) custom-call(f32[1,2,128,32,128]{4,3,2,1,0:T(8,128)} %orb_ref.1), custom_call_target="tpu_custom_call" | custom-call | tf_op jit(solution)/shard_map/split/pallas_call | solution.py:336
  31.1 0.0 copy-start
  31.1 0.0 collective-permute-done.9.theirs_ref
  31.1 1.3 %slab.1.charge_ref = f32[32,128]{1,0:T(8,128)S(1)} custom-call(f32[128,128]{1,0:T(8,128)S(1)} %add.23.mine_ref, f32[128,128]{1,0:T(8,128)S(1)} %collective-permute-done.9.theirs_ref, bf16[32,256,128]{2,1,0:T(8,128)(2,1)S(1)} %get-tuple-element.10.high_ref, f32[32,256,128]{2,1,0:T(8,128)S(1)} %get-tuple-element.11.other_ref), custom_call_target="tpu_custom_call" | custom-call | tf_op jit(solution)/shard_map/slab/pallas_call | solution.py:348
  32.5 0.0 collective-permute-done.6.d_ref
  32.5 0.0 collective-permute-done.5.c_ref
  32.5 0.0 collective-permute-done.4.b_ref
  32.5 0.0 copy-done
  32.5 0.6 %pack.1 = f32[32,16,128]{2,1,0:T(8,128)S(1)} custom-call(s32[32]{0:T(128)S(1)} %copy-done, f32[16,128]{1,0:T(8,128)S(1)} %get-tuple-element.18.a_ref, f32[16,128]{1,0:T(8,128)S(1)} %collective-permute-done.4.b_ref, f32[16,128]{1,0:T(8,128)S(1)} %collective-permute-done.5.c_ref, f32[16,128]{1,0:T(8,128)S(1)} %collective-permute-done.6.d_ref, ...), custom_call_target="tpu_custom_call" | custom-call | tf_op jit(solution)/shard_map/pack/pallas_call | solution.py:356
  33.1 24.2 %all_to_all.5.in_ref = f32[32,16,128]{2,1,0:T(8,128)S(1)} all-to-all(f32[32,16,128]{2,1,0:T(8,128)S(1)} %pack.1), channel_id=1, replica_groups=mesh['ka'=32,'freq'=8] {'ka'}, dimensions={0} | all-to-all | bytes 524288 | tf_op jit(solution)/shard_map/all_to_all | solution.py:364
  57.3 1.0 %unpack.1 = (f32[16,2,40,40]{3,2,1,0:T(8,128)}, f32[1,128]{1,0:T(1,128)}) custom-call(f32[32,16,128]{2,1,0:T(8,128)S(1)} %all_to_all.5.in_ref), custom_call_target="tpu_custom_call" | custom-call | tf_op jit(solution)/shard_map/unpack/pallas_call | solution.py:366
  (6 shorter events, 0.1 us)
Async XLA Ops:
  5.9 7.0 %collective-permute-start = (f32[16,16,128]{2,1,0:T(8,128)S(1)}, f32[16,16,128]{2,1,0:T(8,128)S(1)}, u32[]{:S(2)}, u32[]{:S(2)}) collective-permute-start(f32[16,16,128]{2,1,0:T(8,128)S(1)} %get-tuple-element.8), channel_id=1, source_target_pairs={{0,8},{8,0},{16,24},{24,16},{32,40},{40,32},{48,56},{56,48},{64,72... | collective-permute-start | bytes 393224 | tf_op jit(solution)/shard_map/ppermute | solution.py:322
  9.2 3.5 %collective-permute-start.7 = (f32[128,128]{1,0:T(8,128)S(1)}, f32[128,128]{1,0:T(8,128)S(1)}, u32[]{:S(2)}, u32[]{:S(2)}) collective-permute-start(f32[128,128]{1,0:T(8,128)S(1)} %get-tuple-element.9), channel_id=1, source_target_pairs={{0,4},{1,5},{2,6},{3,7},{4,0},{5,1},{6,2},{7,3},{8,12},{9,13},{10,... | collective-permute-start | bytes 196616 | tf_op jit(solution)/shard_map/ppermute | solution.py:322
  12.8 3.8 %collective-permute-start.8 = (f32[128,128]{1,0:T(8,128)S(1)}, f32[128,128]{1,0:T(8,128)S(1)}, u32[]{:S(2)}, u32[]{:S(2)}) collective-permute-start(f32[128,128]{1,0:T(8,128)S(1)} %add.22), channel_id=1, source_target_pairs={{0,1},{1,0},{2,3},{3,2},{4,5},{5,4},{6,7},{7,6},{8,9},{9,8},{10,11... | collective-permute-start | bytes 196616 | tf_op jit(solution)/shard_map/ppermute | solution.py:322
  12.9 5.5 %collective-permute-start.2 = (f32[4,16,128]{2,1,0:T(8,128)S(1)}, f32[4,16,128]{2,1,0:T(8,128)S(1)}, u32[]{:S(2)}, u32[]{:S(2)}) collective-permute-start(f32[4,16,128]{2,1,0:T(8,128)S(1)} %get-tuple-element.12), channel_id=1, source_target_pairs={{0,32},{8,40},{16,48},{24,56},{32,0},{40,8},{48,16},{56,24},{64,96... | collective-permute-start | bytes 98312 | tf_op jit(solution)/shard_map/ppermute | solution.py:322
  15.8 4.0 %collective-permute-start.3 = (f32[4,16,128]{2,1,0:T(8,128)S(1)}, f32[4,16,128]{2,1,0:T(8,128)S(1)}, u32[]{:S(2)}, u32[]{:S(2)}) collective-permute-start(f32[4,16,128]{2,1,0:T(8,128)S(1)} %get-tuple-element.13), channel_id=1, source_target_pairs={{0,48},{8,56},{16,32},{24,40},{32,16},{40,24},{48,0},{56,8},{64,11... | collective-permute-start | bytes 98312 | tf_op jit(solution)/shard_map/ppermute | solution.py:322
  16.5 3.2 %collective-permute-start.1 = (f32[4,16,128]{2,1,0:T(8,128)S(1)}, f32[4,16,128]{2,1,0:T(8,128)S(1)}, u32[]{:S(2)}, u32[]{:S(2)}) collective-permute-start(f32[4,16,128]{2,1,0:T(8,128)S(1)} %get-tuple-element.14), channel_id=1, source_target_pairs={{0,16},{8,24},{16,0},{24,8},{32,48},{40,56},{48,32},{56,40},{64,80... | collective-permute-start | bytes 98312 | tf_op jit(solution)/shard_map/ppermute | solution.py:322
  16.5 14.6 %collective-permute-start.9 = (f32[128,128]{1,0:T(8,128)S(1)}, f32[128,128]{1,0:T(8,128)S(1)}, u32[]{:S(2)}, u32[]{:S(2)}) collective-permute-start(f32[128,128]{1,0:T(8,128)S(1)} %add.23.mine_ref), channel_id=1, source_target_pairs={{0,3},{1,2},{2,1},{3,0},{4,7},{5,6},{6,5},{7,4},{8,11},{9,10},{10,... | collective-permute-start | bytes 196616 | tf_op jit(solution)/shard_map/ppermute | solution.py:322
  19.8 12.7 %collective-permute-start.6 = (f32[16,128]{1,0:T(8,128)S(1)}, f32[16,128]{1,0:T(8,128)S(1)}, u32[]{:S(2)}, u32[]{:S(2)}) collective-permute-start(f32[16,128]{1,0:T(8,128)S(1)} %get-tuple-element.15), channel_id=1, source_target_pairs={{0,192},{8,200},{16,208},{24,216},{32,224},{40,232},{48,240},{56,2... | collective-permute-start | bytes 24584 | tf_op jit(solution)/shard_map/ppermute | solution.py:322
  25.5 7.0 %collective-permute-start.5 = (f32[16,128]{1,0:T(8,128)S(1)}, f32[16,128]{1,0:T(8,128)S(1)}, u32[]{:S(2)}, u32[]{:S(2)}) collective-permute-start(f32[16,128]{1,0:T(8,128)S(1)} %get-tuple-element.16), channel_id=1, source_target_pairs={{0,128},{8,136},{16,144},{24,152},{32,160},{40,168},{48,176},{56,1... | collective-permute-start | bytes 24584 | tf_op jit(solution)/shard_map/ppermute | solution.py:322
  26.5 6.0 %collective-permute-start.4 = (f32[16,128]{1,0:T(8,128)S(1)}, f32[16,128]{1,0:T(8,128)S(1)}, u32[]{:S(2)}, u32[]{:S(2)}) collective-permute-start(f32[16,128]{1,0:T(8,128)S(1)} %get-tuple-element.17), channel_id=1, source_target_pairs={{0,64},{8,72},{16,80},{24,88},{32,96},{40,104},{48,112},{56,120},{... | collective-permute-start | bytes 24584 | tf_op jit(solution)/shard_map/ppermute | solution.py:322
  31.1 1.4 %copy-start = (s32[32]{0:T(128)S(1)}, s32[32]{0:T(128)}, u32[]{:S(2)}) copy-start(s32[32]{0:T(128)} %owner_ref.1) | copy-start | bytes 388

commit v3 on v1

--- a/solution.py
+++ b/solution.py
@@ -199,8 +199,8 @@
         other_ref[base + s] = 2.0 * x - h.astype(F32)
 
 
-def slab_kernel(mine_ref, theirs_ref, high_ref, other_ref, out_ref):
-    packed = mine_ref[...] + theirs_ref[...]
+def slab_kernel(a_ref, b_ref, c_ref, d_ref, high_ref, other_ref, out_ref):
+    packed = (a_ref[...] + b_ref[...]) + (c_ref[...] + d_ref[...])
     packed_t = packed.T
     row = lax.broadcasted_iota(jnp.int32, packed.shape, 0)
     col = lax.broadcasted_iota(jnp.int32, packed.shape, 1)
@@ -305,8 +305,7 @@
     theirs = swapped(dens, 4)
     rows_in = lax.all_to_all(rows, "ka", 0, 0, tiled=True)
     dens = dens + theirs
-    dens = dens + swapped(dens, 1)
-    theirs = swapped(dens, 3)
+    arrived = [swapped(dens, d) for d in range(1, 4)]
 
     step = 8
     high, other = pl.pallas_call(
@@ -321,15 +320,14 @@
         compiler_params=pltpu.CompilerParams(vmem_limit_bytes=8 << 20),
         name="split",
     )(far(orbitals))
-
     rho = pl.pallas_call(
         slab_kernel,
         out_shape=pltpu.VMEM((slabs, LANES), F32),
-        in_specs=[whole()] * 4,
+        in_specs=[whole()] * 6,
         out_specs=whole(),
         compiler_params=pltpu.CompilerParams(vmem_limit_bytes=8 << 20),
         name="slab",
-    )(held(dens), held(theirs), held(high), held(other))
+    )(*[held(x) for x in (dens, *arrived, high, other)])
     sends = pl.pallas_call(
         pack_kernel,
         out_shape=pltpu.VMEM((peers, PIECE, LANES), F32),

time: 65 us -> 62.9 us (0.968)
  waiting for transfers between devices: 10.2 us -> 8.44 us
    ppermute x3 -> x4, waiting for transfers between devices: 10.2 us -> 8.43 us  [swapped(): return lax.ppermute(x, 'freq', [(i, i ^ flip) for i in range(poles)])]
    ppermute x3 -> x4, starting transfers between devices: 4.68 us -> 4.17 us  [swapped(): return lax.ppermute(x, 'freq', [(i, i ^ flip) for i in range(poles)])]
  transfers between devices with their start and end apart: 4 -> 5, of which waited for: 2 -> 2; matrix products, arithmetic and copies ran while one was open for 0% -> 0% of each run, Pallas kernels for 7% -> 8%
where the time goes in v3:
time: 62.9 us; the launch traced here: 62.6 us
  blocking collectives  24.2 us (38%)
  starting transfers between devices  16.9 us (27%)
  Pallas kernels  11.7 us (19%)
  waiting for transfers between devices  8.44 us (13%)
  between operations  1.35 us (2%)
    all_to_all x1, blocking collectives, local(): back = lax.all_to_all(sends, 'ka', 0, 0, tiled=True)  24.2 us
    all_to_all x1, starting transfers between devices, local(): rows_in = lax.all_to_all(rows, 'ka', 0, 0, tiled=True)  12.8 us
    ppermute x4, waiting for transfers between devices, swapped(): return lax.ppermute(x, 'freq', [(i, i ^ flip) for i in range(poles)])  8.43 us
    pallas_call x1, Pallas kernels, local(): pl.pallas_call(green_kernel(pole_total, n, poles, thermal_level), out_sha...  5.31 us
    ppermute x4, starting transfers between devices, swapped(): return lax.ppermute(x, 'freq', [(i, i ^ flip) for i in range(poles)])  4.17 us
    pallas_call x1, Pallas kernels, local(): pl.pallas_call(split_kernel, grid=(slabs // step,), in_specs=[pl.BlockSpe...  3.42 us
    pallas_call x1, Pallas kernels, local(): pl.pallas_call(slab_kernel, out_shape=pltpu.VMEM((slabs, LANES), F32), in...  1.31 us
  transfers between devices with their start and end apart: 5, of which 2 were waited for; matrix products, arithmetic and copies ran while one was open for 0% of the time, Pallas kernels for 8%

profile of v3, /device:TPU:1, one launch (start us, length us, event | category | flops | bytes accessed | tf_op | source)
XLA Modules:
  0.0 62.6 jit_solution(9447048812015691800)
XLA Ops:
  1.3 5.3 %green.1 = (f32[128,128]{1,0:T(8,128)S(1)}, f32[32,16,128]{2,1,0:T(8,128)}) custom-call(s32[1]{0:T(128)S(6)} %copy.9.mult_ref, f32[1,128]{1,0:T(1,128)} %energy_ref.1, f32[1,2,40,128]{3,2,1,0:T(8,128)} %bitcast.1, f32[16,2,40,40]{3,2,1,0:T(8,128)} %self_hbm.1, f32[40,40]{1,0:T(8,128)} %rot_ref.1), custom_call_target="tpu_custom_call" | custom-call | tf_op jit(solution)/shard_map/green/pallas_call | solution.py:279
  6.6 12.8 %all-to-all-start = ((f32[32,16,128]{2,1,0:T(8,128)}), f32[32,16,128]{2,1,0:T(8,128)S(1)}, u32[]{:S(2)}, u32[]{:S(2)}) async-start(f32[32,16,128]{2,1,0:T(8,128)} %get-tuple-element.6), calls=%async_computation | async-start | bytes 524288 | tf_op jit(solution)/shard_map/all_to_all | solution.py:306
  19.4 0.8 %collective-permute-start = (f32[128,128]{1,0:T(8,128)S(1)}, f32[128,128]{1,0:T(8,128)S(1)}, u32[]{:S(2)}, u32[]{:S(2)}) collective-permute-start(f32[128,128]{1,0:T(8,128)S(1)} %get-tuple-element.7), channel_id=1, source_target_pairs={{0,4},{1,5},{2,6},{3,7},{4,0},{5,1},{6,2},{7,3},{8,12},{9,13},{10,... | collective-permute-start | bytes 196616 | tf_op jit(solution)/shard_map/ppermute | solution.py:303
  20.2 8.0 %collective-permute-done = f32[128,128]{1,0:T(8,128)S(1)} collective-permute-done((f32[128,128]{1,0:T(8,128)S(1)}, f32[128,128]{1,0:T(8,128)S(1)}, u32[]{:S(2)}, u32[]{:S(2)}) %collective-permute-start) | collective-permute-done | bytes 65568 | tf_op jit(solution)/shard_map/ppermute | solution.py:303
  28.2 2.6 %collective-permute-start.3 = (f32[128,128]{1,0:T(8,128)S(1)}, f32[128,128]{1,0:T(8,128)S(1)}, u32[]{:S(2)}, u32[]{:S(2)}) collective-permute-start(f32[128,128]{1,0:T(8,128)S(1)} %add.3.a_ref), channel_id=1, source_target_pairs={{0,3},{1,2},{2,1},{3,0},{4,7},{5,6},{6,5},{7,4},{8,11},{9,10},{10,... | collective-permute-start | bytes 196616 | tf_op jit(solution)/shard_map/ppermute | solution.py:303
  30.8 0.5 collective-permute-start.2
  31.3 0.3 collective-permute-start.1
  31.6 3.4 %split.1 = (bf16[32,256,128]{2,1,0:T(8,128)(2,1)S(1)}, f32[32,256,128]{2,1,0:T(8,128)S(1)}) custom-call(f32[1,2,128,32,128]{4,3,2,1,0:T(8,128)} %orb_ref.1), custom_call_target="tpu_custom_call" | custom-call | tf_op jit(solution)/shard_map/split/pallas_call | solution.py:311
  35.0 0.0 copy-start
  35.0 0.0 collective-permute-done.3.d_ref
  35.0 0.4 collective-permute-done.2.c_ref
  35.4 0.0 collective-permute-done.1.b_ref
  35.4 1.3 %slab.1.charge_ref = f32[32,128]{1,0:T(8,128)S(1)} custom-call(f32[128,128]{1,0:T(8,128)S(1)} %add.3.a_ref, f32[128,128]{1,0:T(8,128)S(1)} %collective-permute-done.1.b_ref, f32[128,128]{1,0:T(8,128)S(1)} %collective-permute-done.2.c_ref, f32[128,128]{1,0:T(8,128)S(1)} %collective-permute-done.3.d_ref, bf16[32,256,128]{2,1,0:T(8,128)(2,1)S(1)} %get-tuple-element.8.high_ref, ...), custom_call_target="tpu_custom_call" | custom-call | tf_op jit(solution)/shard_map/slab/pallas_call | solution.py:323
  36.7 0.0 all-to-all-done.local_ref
  36.7 0.0 copy-done
  36.8 0.6 pack.1
  37.4 24.2 %all_to_all.10.in_ref = f32[32,16,128]{2,1,0:T(8,128)S(1)} all-to-all(f32[32,16,128]{2,1,0:T(8,128)S(1)} %pack.1), channel_id=1, replica_groups=mesh['ka'=32,'freq'=8] {'ka'}, dimensions={0} | all-to-all | bytes 524288 | tf_op jit(solution)/shard_map/all_to_all | solution.py:339
  61.5 1.0 %unpack.1 = (f32[16,2,40,40]{3,2,1,0:T(8,128)}, f32[1,128]{1,0:T(1,128)}) custom-call(f32[32,16,128]{2,1,0:T(8,128)S(1)} %all_to_all.10.in_ref), custom_call_target="tpu_custom_call" | custom-call | tf_op jit(solution)/shard_map/unpack/pallas_call | solution.py:341
  (1 shorter events, 0.0 us)
Async XLA Ops:
  6.6 30.1 %all-to-all-start = ((f32[32,16,128]{2,1,0:T(8,128)}), f32[32,16,128]{2,1,0:T(8,128)S(1)}, u32[]{:S(2)}, u32[]{:S(2)}) async-start(f32[32,16,128]{2,1,0:T(8,128)} %get-tuple-element.6), calls=%async_computation | async-start | bytes 524288 | tf_op jit(solution)/shard_map/all_to_all | solution.py:306
  19.4 8.9 %collective-permute-start = (f32[128,128]{1,0:T(8,128)S(1)}, f32[128,128]{1,0:T(8,128)S(1)}, u32[]{:S(2)}, u32[]{:S(2)}) collective-permute-start(f32[128,128]{1,0:T(8,128)S(1)} %get-tuple-element.7), channel_id=1, source_target_pairs={{0,4},{1,5},{2,6},{3,7},{4,0},{5,1},{6,2},{7,3},{8,12},{9,13},{10,... | collective-permute-start | bytes 196616 | tf_op jit(solution)/shard_map/ppermute | solution.py:303
  28.2 6.8 %collective-permute-start.3 = (f32[128,128]{1,0:T(8,128)S(1)}, f32[128,128]{1,0:T(8,128)S(1)}, u32[]{:S(2)}, u32[]{:S(2)}) collective-permute-start(f32[128,128]{1,0:T(8,128)S(1)} %add.3.a_ref), channel_id=1, source_target_pairs={{0,3},{1,2},{2,1},{3,0},{4,7},{5,6},{6,5},{7,4},{8,11},{9,10},{10,... | collective-permute-start | bytes 196616 | tf_op jit(solution)/shard_map/ppermute | solution.py:303
  30.8 4.6 %collective-permute-start.2 = (f32[128,128]{1,0:T(8,128)S(1)}, f32[128,128]{1,0:T(8,128)S(1)}, u32[]{:S(2)}, u32[]{:S(2)}) collective-permute-start(f32[128,128]{1,0:T(8,128)S(1)} %add.3.a_ref), channel_id=1, source_target_pairs={{0,2},{1,3},{2,0},{3,1},{4,6},{5,7},{6,4},{7,5},{8,10},{9,11},{10,... | collective-permute-start | bytes 196616 | tf_op jit(solution)/shard_map/ppermute | solution.py:303
  31.3 4.1 %collective-permute-start.1 = (f32[128,128]{1,0:T(8,128)S(1)}, f32[128,128]{1,0:T(8,128)S(1)}, u32[]{:S(2)}, u32[]{:S(2)}) collective-permute-start(f32[128,128]{1,0:T(8,128)S(1)} %add.3.a_ref), channel_id=1, source_target_pairs={{0,1},{1,0},{2,3},{3,2},{4,5},{5,4},{6,7},{7,6},{8,9},{9,8},{10,11... | collective-permute-start | bytes 196616 | tf_op jit(solution)/shard_map/ppermute | solution.py:303
  35.0 1.8 %copy-start = (s32[32]{0:T(128)S(1)}, s32[32]{0:T(128)}, u32[]{:S(2)}) copy-start(s32[32]{0:T(128)} %owner_ref.1) | copy-start | bytes 388

commit v4 on v2

--- a/solution.py
+++ b/solution.py
@@ -13,6 +13,7 @@
 LANES = 128
 WIDE = 3
 PIECE = 16
+USED = 13
 
 
 def low(x):
@@ -183,23 +184,29 @@
         scale = weight * thermal_level
         dens_ref[...] = scale * jnp.where(row <= col, er + er.T, ei - ei.T)
 
+        outs = []
         for g in range(groups):
             out = both_right[g] + mm3(
                 a1_left[g] + last[g][n:], *block_weights(small_right[g], masks)
             )
             out = weight * out
-            flat_ref[2 * n * g : 2 * n * g + n, :] = out[:, :LANES]
-            flat_ref[2 * n * g + n : 2 * n * (g + 1), :] = out[:, LANES:]
-        per = PIECE - 1
+            outs.append(jnp.concatenate([out[:, :LANES], out[:, LANES:]], axis=0))
+        spare = LANES - WIDE * n
+        wide_lane = lax.broadcasted_iota(jnp.int32, (2 * n, LANES), 1)
+        for g in range(groups - 1):
+            moved = pltpu.roll(outs[-1], LANES - spare * (g + 1), 1)
+            flat_ref[2 * n * g : 2 * n * (g + 1), :] = jnp.where(
+                wide_lane < WIDE * n, outs[g], moved
+            )
+        rows = 2 * n * (groups - 1)
+        flat_ref[rows:, :] = jnp.zeros((flat_ref.shape[0] - rows, LANES), F32)
         for d in range(rows_ref.shape[0]):
-            rows_ref[d, 0:per, :] = flat_ref[per * d : per * (d + 1), :]
-            rows_ref[d, per:PIECE, :] = jnp.broadcast_to(weight, (1, LANES))
-        me = lax.axis_index("ka")
-        half = keep_ref.shape[0]
-        for r in range(half):
-            d = ((r % 4) * 8 + (r // 4) * 2) ^ me
-            keep_ref[r] = rows_ref[d]
-            give_ref[r] = rows_ref[d ^ 1]
+            rows_ref[d, 0:USED, :] = flat_ref[USED * d : USED * (d + 1), :]
+            rows_ref[d, USED:PIECE, :] = jnp.broadcast_to(weight, (PIECE - USED, LANES))
+        core = lax.axis_index("ka") % 2
+        for r in range(keep_ref.shape[0]):
+            keep_ref[r] = rows_ref[2 * r + core]
+            give_ref[r] = rows_ref[2 * r + 1 - core]
 
     return kernel
 
@@ -239,32 +246,44 @@
             out_ref[s + t : s + t + 1, :] = rho
 
 
-def pack_kernel(owner_ref, a_ref, b_ref, c_ref, d_ref, charge_ref, out_ref):
-    sums = (a_ref[...] + b_ref[...]) + (c_ref[...] + d_ref[...])
-    inverse = 1.0 / sums[PIECE - 1 : PIECE, :]
+def pack_kernel(owner_ref, local_ref, charge_ref, out_ref):
+    sums = jnp.sum(local_ref[...], axis=0)
+    inverse = 1.0 / sums[USED : USED + 1, :]
     sums = sums * inverse
     for d in range(out_ref.shape[0]):
         out_ref[d] = sums
     for s in range(charge_ref.shape[0]):
-        out_ref[owner_ref[s], PIECE - 1 : PIECE, :] = charge_ref[s : s + 1, :] * inverse
+        own = owner_ref[s]
+        out_ref[own // 2, pl.ds(USED + own % 2, 1), :] = charge_ref[s : s + 1, :] * inverse
 
 
 def unpack_kernel(pole_total, orbital_count):
     n = orbital_count
 
-    def kernel(in_ref, green_ref, charge_ref, flat_ref):
-        per = PIECE - 1
+    def kernel(mine_ref, theirs_ref, green_ref, charge_ref, rows_ref, flat_ref):
+        core = lax.axis_index("ka") % 2
+        pieces = mine_ref.shape[0]
         total = None
-        for d in range(in_ref.shape[0]):
-            flat_ref[per * d : per * (d + 1), :] = in_ref[d, 0:per, :]
-            own = in_ref[d, per:PIECE, :]
-            total = own if total is None else total + own
-        charge_ref[...] = total
-        for q in range(pole_total):
+        for r in range(pieces):
+            rows_ref[2 * r + core] = mine_ref[r]
+            rows_ref[2 * r + 1 - core] = theirs_ref[r]
+            both = mine_ref[r, USED : USED + 2, :] + theirs_ref[r, USED : USED + 2, :]
+            total = both if total is None else total + both
+        charge_ref[...] = jnp.where(core == 0, total[0:1], total[1:2])
+        for d in range(2 * pieces):
+            flat_ref[USED * d : USED * (d + 1), :] = rows_ref[d, 0:USED, :]
+        for q in range(pole_total - 1):
             g, j = divmod(q, WIDE)
             for c in range(2):
                 base = n * (2 * g + c)
                 green_ref[q, c] = flat_ref[base : base + n, n * j : n * (j + 1)]
+        spare = LANES - WIDE * n
+        for c in range(2):
+            parts = [
+                flat_ref[n * (2 * g + c) : n * (2 * g + c + 1), WIDE * n :]
+                for g in range(n // spare)
+            ]
+            green_ref[pole_total - 1, c] = jnp.concatenate(parts, axis=1)
 
     return kernel
 
@@ -290,15 +309,17 @@
     bands = projector.shape[2]
     thermal_level = 0.25 / (pole_total * poles)
     groups = -(-pole_total // WIDE)
-    flat_rows = 2 * n * groups
-    assert flat_rows == (PIECE - 1) * peers and bands == LANES
+    flat_rows = USED * peers
+    assert flat_rows >= 2 * n * (groups - 1) and bands == LANES
+    assert pole_total == WIDE * (groups - 1) + 1 and (LANES - WIDE * n) * (groups - 1) == n
+    chips = peers // 2
 
     dens, keep, give = pl.pallas_call(
         green_kernel(pole_total, n, poles, thermal_level),
         out_shape=(
             pltpu.VMEM((bands, bands), F32),
-            pltpu.VMEM((peers // 2, PIECE, LANES), F32),
-            pltpu.VMEM((peers // 2, PIECE, LANES), F32),
+            pltpu.VMEM((chips, PIECE, LANES), F32),
+            pltpu.VMEM((chips, PIECE, LANES), F32),
         ),
         in_specs=[whole(pltpu.SMEM), whole(), whole(), whole(pl.ANY), whole()],
         out_specs=(whole(), whole(), whole()),
@@ -321,16 +342,16 @@
     def swapped(x, axis, flip):
         return lax.ppermute(x, axis, [(i, i ^ flip) for i in range(lax.axis_size(axis))])
 
-    theirs = swapped(give, "ka", 1)
-    other_dens = swapped(dens, "freq", 4)
-    rows = (keep + theirs).reshape(4, 4, PIECE, LANES)
-    arrived = [swapped(rows[d], "ka", 2 * d) for d in range(1, 4)]
-    rows = rows[0] + sum(arrived)
-    dens = dens + other_dens
-    other_dens = swapped(dens, "freq", 1)
-    dens = dens + other_dens
-    parts = [rows[0]] + [swapped(rows[d], "ka", 8 * d) for d in range(1, 4)]
-    theirs = swapped(dens, "freq", 3)
+    def across_chips(x):
+        same_core = [[2 * i + c for i in range(chips)] for c in range(2)]
+        return lax.all_to_all(x, "ka", 0, 0, axis_index_groups=same_core, tiled=True)
+
+    given = swapped(give, "ka", 1)
+    arrived = [swapped(dens, "freq", d) for d in range(1, 4)]
+    rows = keep + given
+    rows_in = across_chips(rows)
+    dens = (dens + arrived[0]) + (arrived[1] + arrived[2])
+    theirs = swapped(dens, "freq", 4)
 
     step = 8
     high, other = pl.pallas_call(
@@ -352,16 +373,17 @@
         out_specs=whole(),
         compiler_params=pltpu.CompilerParams(vmem_limit_bytes=8 << 20),
         name="slab",
-    )(held(dens), held(theirs), held(high), held(other))
+    )(*[held(x) for x in (dens, theirs, high, other)])
     sends = pl.pallas_call(
         pack_kernel,
-        out_shape=pltpu.VMEM((peers, PIECE, LANES), F32),
-        in_specs=[whole(pltpu.SMEM)] + [whole()] * 5,
+        out_shape=pltpu.VMEM((chips, PIECE, LANES), F32),
+        in_specs=[whole(pltpu.SMEM), whole(), whole()],
         out_specs=whole(),
         compiler_params=pltpu.CompilerParams(vmem_limit_bytes=4 << 20),
         name="pack",
-    )(owner, *[held(x) for x in parts], held(rho))
-    back = lax.all_to_all(sends, "ka", 0, 0, tiled=True)
+    )(owner, held(rows_in), held(rho))
+    back = across_chips(sends)
+    across = swapped(back, "ka", 1)
 
     local_green, slab = pl.pallas_call(
         unpack_kernel(pole_total, n),
@@ -369,12 +391,15 @@
             jax.ShapeDtypeStruct((pole_total, 2, n, n), F32),
             jax.ShapeDtypeStruct((1, LANES), F32),
         ),
-        in_specs=[whole()],
+        in_specs=[whole(), whole()],
         out_specs=(whole(), whole()),
-        scratch_shapes=[pltpu.VMEM((flat_rows, LANES), F32)],
+        scratch_shapes=[
+            pltpu.VMEM((peers, PIECE, LANES), F32),
+            pltpu.VMEM((flat_rows, LANES), F32),
+        ],
         compiler_params=pltpu.CompilerParams(vmem_limit_bytes=6 << 20),
         name="unpack",
-    )(held(back))
+    )(held(back), held(across))
     return (local_green, slab)
 
 

time: 58.6 us -> 53.2 us (0.908)
  blocking collectives: 24.2 us -> 15.2 us
  starting transfers between devices: 16.8 us -> 19.6 us
  other arithmetic: 0.05 us -> 0.69 us
    all_to_all x0 -> x1, starting transfers between devices: none -> 9.21 us  [across_chips(): lax.all_to_all(x, 'ka', 0, 0, axis_index_groups=same_core, tiled=True)]
    all_to_all x1, blocking collectives: 24.2 us -> 15.2 us  [across_chips(): lax.all_to_all(x, 'ka', 0, 0, axis_index_groups=same_core, tiled=True)]
    ppermute x10 -> x6, starting transfers between devices: 16.8 us -> 10.4 us  [swapped(): lax.ppermute(x, axis, [(i, i ^ flip) for i in range(lax.axis_size(axis))])]
    ppermute x10 -> x6, waiting for transfers between devices: 4.84 us -> 1 us  [swapped(): lax.ppermute(x, axis, [(i, i ^ flip) for i in range(lax.axis_size(axis))])]
    all_to_all x0 -> x1, waiting for transfers between devices: none -> 3.6 us  [across_chips(): lax.all_to_all(x, 'ka', 0, 0, axis_index_groups=same_core, tiled=True)]
    add x4 -> x2, other arithmetic: 0.05 us -> 0.69 us  [the longest x1 0.67 us: local(): rows = keep + given]
  transfers between devices with their start and end apart: 10 -> 7, of which waited for: 2 -> 2; matrix products, arithmetic and copies ran while one was open for 0% -> 1% of each run, Pallas kernels for 8% -> 9%
where the time goes in v4:
time: 53.2 us; the launch traced here: 52.8 us
  starting transfers between devices  19.6 us (37%)
  blocking collectives  15.2 us (29%)
  Pallas kernels  11.3 us (21%)
  waiting for transfers between devices  4.6 us (9%)
  between operations  1.37 us (3%)
  other arithmetic  0.69 us (1%)
    all_to_all x1, blocking collectives, across_chips(): lax.all_to_all(x, 'ka', 0, 0, axis_index_groups=same_core, tiled=True)  15.2 us
    ppermute x6, starting transfers between devices, swapped(): lax.ppermute(x, axis, [(i, i ^ flip) for i in range(lax.axis_size(axis))])  10.4 us
    all_to_all x1, starting transfers between devices, across_chips(): lax.all_to_all(x, 'ka', 0, 0, axis_index_groups=same_core, tiled=True)  9.21 us
    pallas_call x1, Pallas kernels, local(): pl.pallas_call(green_kernel(pole_total, n, poles, thermal_level), out_sha...  4.75 us
    all_to_all x1, waiting for transfers between devices, across_chips(): lax.all_to_all(x, 'ka', 0, 0, axis_index_groups=same_core, tiled=True)  3.6 us
    pallas_call x1, Pallas kernels, local(): pl.pallas_call(split_kernel, grid=(slabs // step,), in_specs=[pl.BlockSpe...  3.42 us
    pallas_call x1, Pallas kernels, local(): pl.pallas_call(slab_kernel, out_shape=pltpu.VMEM((slabs, LANES), F32), in...  1.3 us
    pallas_call x1, Pallas kernels, local(): pl.pallas_call(unpack_kernel(pole_total, n), out_shape=(jax.ShapeDtypeStr...  1.12 us
  transfers between devices with their start and end apart: 7, of which 2 were waited for; matrix products, arithmetic and copies ran while one was open for 1% of the time, Pallas kernels for 9%

profile of v4, /device:TPU:1, one launch (start us, length us, event | category | flops | bytes accessed | tf_op | source)
XLA Modules:
  0.0 52.8 jit_solution(18434717991483642340)
XLA Ops:
  1.3 4.7 %green.1 = (f32[128,128]{1,0:T(8,128)S(1)}, f32[16,16,128]{2,1,0:T(8,128)S(1)}, f32[16,16,128]{2,1,0:T(8,128)S(1)}) custom-call(s32[1]{0:T(128)S(6)} %copy.9.mult_ref, f32[1,128]{1,0:T(1,128)} %energy_ref.1, f32[1,2,40,128]{3,2,1,0:T(8,128)} %bitcast.1, f32[16,2,40,40]{3,2,1,0:T(8,128)} %self_hbm.1, f32[40,40]{1,0:T(8,128)} %rot_ref.1), custom_call_target="tpu_custom_call" | custom-call | tf_op jit(solution)/shard_map/green/pallas_call | solution.py:317
  6.0 3.3 %collective-permute-start = (f32[16,16,128]{2,1,0:T(8,128)S(1)}, f32[16,16,128]{2,1,0:T(8,128)S(1)}, u32[]{:S(2)}, u32[]{:S(2)}) collective-permute-start(f32[16,16,128]{2,1,0:T(8,128)S(1)} %get-tuple-element.8), channel_id=1, source_target_pairs={{0,8},{8,0},{16,24},{24,16},{32,40},{40,32},{48,56},{56,48},{64,72... | collective-permute-start | bytes 393224 | tf_op jit(solution)/shard_map/ppermute | solution.py:343
  9.3 0.8 %collective-permute-start.3 = (f32[128,128]{1,0:T(8,128)S(1)}, f32[128,128]{1,0:T(8,128)S(1)}, u32[]{:S(2)}, u32[]{:S(2)}) collective-permute-start(f32[128,128]{1,0:T(8,128)S(1)} %get-tuple-element.9), channel_id=1, source_target_pairs={{0,3},{1,2},{2,1},{3,0},{4,7},{5,6},{6,5},{7,4},{8,11},{9,10},{10,... | collective-permute-start | bytes 196616 | tf_op jit(solution)/shard_map/ppermute | solution.py:343
  10.1 0.5 collective-permute-start.2
  10.6 2.0 %collective-permute-start.1 = (f32[128,128]{1,0:T(8,128)S(1)}, f32[128,128]{1,0:T(8,128)S(1)}, u32[]{:S(2)}, u32[]{:S(2)}) collective-permute-start(f32[128,128]{1,0:T(8,128)S(1)} %get-tuple-element.9), channel_id=1, source_target_pairs={{0,1},{1,0},{2,3},{3,2},{4,5},{5,4},{6,7},{7,6},{8,9},{9,8},{10,11... | collective-permute-start | bytes 196616 | tf_op jit(solution)/shard_map/ppermute | solution.py:343
  12.6 0.0 collective-permute-done
  12.6 0.7 %add.12 = f32[16,16,128]{2,1,0:T(8,128)} add(f32[16,16,128]{2,1,0:T(8,128)S(1)} %get-tuple-element.7, f32[16,16,128]{2,1,0:T(8,128)S(1)} %collective-permute-done) | non-fusion elementwise | flops 32768 | bytes 393216 | tf_op jit(solution)/shard_map/add | solution.py:351
  13.3 9.2 %all-to-all-start = ((f32[16,16,128]{2,1,0:T(8,128)}), f32[16,16,128]{2,1,0:T(8,128)S(1)}, u32[]{:S(2)}, u32[]{:S(2)}) async-start(f32[16,16,128]{2,1,0:T(8,128)} %add.12), calls=%async_computation | async-start | bytes 262144 | tf_op jit(solution)/shard_map/all_to_all | solution.py:347
  22.5 0.0 collective-permute-done.3
  22.5 0.0 collective-permute-done.2
  22.5 0.0 collective-permute-done.1
  22.5 0.8 %collective-permute-start.4 = (f32[128,128]{1,0:T(8,128)S(1)}, f32[128,128]{1,0:T(8,128)S(1)}, u32[]{:S(2)}, u32[]{:S(2)}) collective-permute-start(f32[128,128]{1,0:T(8,128)S(1)} %add_add_fusion.mine_ref), channel_id=1, source_target_pairs={{0,4},{1,5},{2,6},{3,7},{4,0},{5,1},{6,2},{7,3},{8,12},{9,13},{10,... | collective-permute-start | bytes 196616 | tf_op jit(solution)/shard_map/ppermute | solution.py:343
  23.4 3.4 %split.1 = (bf16[32,256,128]{2,1,0:T(8,128)(2,1)S(1)}, f32[32,256,128]{2,1,0:T(8,128)S(1)}) custom-call(f32[1,2,128,32,128]{4,3,2,1,0:T(8,128)} %orb_ref.1), custom_call_target="tpu_custom_call" | custom-call | tf_op jit(solution)/shard_map/split/pallas_call | solution.py:357
  26.8 0.0 copy-start
  26.8 0.0 collective-permute-done.4.theirs_ref
  26.8 1.3 %slab.1.charge_ref = f32[32,128]{1,0:T(8,128)S(1)} custom-call(f32[128,128]{1,0:T(8,128)S(1)} %add_add_fusion.mine_ref, f32[128,128]{1,0:T(8,128)S(1)} %collective-permute-done.4.theirs_ref, bf16[32,256,128]{2,1,0:T(8,128)(2,1)S(1)} %get-tuple-element.10.high_ref, f32[32,256,128]{2,1,0:T(8,128)S(1)} %get-tuple-element.11.other_ref), custom_call_target="tpu_custom_call" | custom-call | tf_op jit(solution)/shard_map/slab/pallas_call | solution.py:369
  28.1 3.6 %all-to-all-done.local_ref = f32[16,16,128]{2,1,0:T(8,128)S(1)} async-done(((f32[16,16,128]{2,1,0:T(8,128)}), f32[16,16,128]{2,1,0:T(8,128)S(1)}, u32[]{:S(2)}, u32[]{:S(2)}) %all-to-all-start) | async-done | bytes 131104 | tf_op jit(solution)/shard_map/all_to_all | solution.py:347
  31.7 0.0 copy-done
  31.7 0.7 %pack.1 = f32[16,16,128]{2,1,0:T(8,128)S(1)} custom-call(s32[32]{0:T(128)S(1)} %copy-done, f32[16,16,128]{2,1,0:T(8,128)S(1)} %all-to-all-done.local_ref, f32[32,128]{1,0:T(8,128)S(1)} %slab.1.charge_ref), custom_call_target="tpu_custom_call" | custom-call | tf_op jit(solution)/shard_map/pack/pallas_call | solution.py:377
  32.5 15.2 %all_to_all.10.mine_ref = f32[16,16,128]{2,1,0:T(8,128)S(1)} all-to-all(f32[16,16,128]{2,1,0:T(8,128)S(1)} %pack.1), channel_id=1, replica_groups={{0,16,32,48,64,80,96,112,128,144,160,176,192,208,224,240},{8,24,40,56,7..., dimensions={0} | all-to-all | bytes 262144 | tf_op jit(solution)/shard_map/all_to_all | solution.py:347
  47.7 3.0 %collective-permute-start.5 = (f32[16,16,128]{2,1,0:T(8,128)S(1)}, f32[16,16,128]{2,1,0:T(8,128)S(1)}, u32[]{:S(2)}, u32[]{:S(2)}) collective-permute-start(f32[16,16,128]{2,1,0:T(8,128)S(1)} %all_to_all.10.mine_ref), channel_id=1, source_target_pairs={{0,8},{8,0},{16,24},{24,16},{32,40},{40,32},{48,56},{56,48},{64,72... | collective-permute-start | bytes 393224 | tf_op jit(solution)/shard_map/ppermute | solution.py:343
  50.7 1.0 %collective-permute-done.5.theirs_ref = f32[16,16,128]{2,1,0:T(8,128)S(1)} collective-permute-done((f32[16,16,128]{2,1,0:T(8,128)S(1)}, f32[16,16,128]{2,1,0:T(8,128)S(1)}, u32[]{:S(2)}, u32[]{:S(2)}) %collective-permute-start.5) | collective-permute-done | bytes 131104 | tf_op jit(solution)/shard_map/ppermute | solution.py:343
  51.7 1.1 %unpack.1 = (f32[16,2,40,40]{3,2,1,0:T(8,128)}, f32[1,128]{1,0:T(1,128)}) custom-call(f32[16,16,128]{2,1,0:T(8,128)S(1)} %all_to_all.10.mine_ref, f32[16,16,128]{2,1,0:T(8,128)S(1)} %collective-permute-done.5.theirs_ref), custom_call_target="tpu_custom_call" | custom-call | tf_op jit(solution)/shard_map/unpack/pallas_call | solution.py:388
  (1 shorter events, 0.0 us)
Async XLA Ops:
  6.0 6.5 %collective-permute-start = (f32[16,16,128]{2,1,0:T(8,128)S(1)}, f32[16,16,128]{2,1,0:T(8,128)S(1)}, u32[]{:S(2)}, u32[]{:S(2)}) collective-permute-start(f32[16,16,128]{2,1,0:T(8,128)S(1)} %get-tuple-element.8), channel_id=1, source_target_pairs={{0,8},{8,0},{16,24},{24,16},{32,40},{40,32},{48,56},{56,48},{64,72... | collective-permute-start | bytes 393224 | tf_op jit(solution)/shard_map/ppermute | solution.py:343
  9.3 13.2 %collective-permute-start.3 = (f32[128,128]{1,0:T(8,128)S(1)}, f32[128,128]{1,0:T(8,128)S(1)}, u32[]{:S(2)}, u32[]{:S(2)}) collective-permute-start(f32[128,128]{1,0:T(8,128)S(1)} %get-tuple-element.9), channel_id=1, source_target_pairs={{0,3},{1,2},{2,1},{3,0},{4,7},{5,6},{6,5},{7,4},{8,11},{9,10},{10,... | collective-permute-start | bytes 196616 | tf_op jit(solution)/shard_map/ppermute | solution.py:343
  10.1 12.4 %collective-permute-start.2 = (f32[128,128]{1,0:T(8,128)S(1)}, f32[128,128]{1,0:T(8,128)S(1)}, u32[]{:S(2)}, u32[]{:S(2)}) collective-permute-start(f32[128,128]{1,0:T(8,128)S(1)} %get-tuple-element.9), channel_id=1, source_target_pairs={{0,2},{1,3},{2,0},{3,1},{4,6},{5,7},{6,4},{7,5},{8,10},{9,11},{10,... | collective-permute-start | bytes 196616 | tf_op jit(solution)/shard_map/ppermute | solution.py:343
  10.6 11.9 %collective-permute-start.1 = (f32[128,128]{1,0:T(8,128)S(1)}, f32[128,128]{1,0:T(8,128)S(1)}, u32[]{:S(2)}, u32[]{:S(2)}) collective-permute-start(f32[128,128]{1,0:T(8,128)S(1)} %get-tuple-element.9), channel_id=1, source_target_pairs={{0,1},{1,0},{2,3},{3,2},{4,5},{5,4},{6,7},{7,6},{8,9},{9,8},{10,11... | collective-permute-start | bytes 196616 | tf_op jit(solution)/shard_map/ppermute | solution.py:343
  13.3 18.5 %all-to-all-start = ((f32[16,16,128]{2,1,0:T(8,128)}), f32[16,16,128]{2,1,0:T(8,128)S(1)}, u32[]{:S(2)}, u32[]{:S(2)}) async-start(f32[16,16,128]{2,1,0:T(8,128)} %add.12), calls=%async_computation | async-start | bytes 262144 | tf_op jit(solution)/shard_map/all_to_all | solution.py:347
  22.5 4.3 %collective-permute-start.4 = (f32[128,128]{1,0:T(8,128)S(1)}, f32[128,128]{1,0:T(8,128)S(1)}, u32[]{:S(2)}, u32[]{:S(2)}) collective-permute-start(f32[128,128]{1,0:T(8,128)S(1)} %add_add_fusion.mine_ref), channel_id=1, source_target_pairs={{0,4},{1,5},{2,6},{3,7},{4,0},{5,1},{6,2},{7,3},{8,12},{9,13},{10,... | collective-permute-start | bytes 196616 | tf_op jit(solution)/shard_map/ppermute | solution.py:343
  26.8 4.9 %copy-start = (s32[32]{0:T(128)S(1)}, s32[32]{0:T(128)}, u32[]{:S(2)}) copy-start(s32[32]{0:T(128)} %owner_ref.1) | copy-start | bytes 388
  47.7 4.0 %collective-permute-start.5 = (f32[16,16,128]{2,1,0:T(8,128)S(1)}, f32[16,16,128]{2,1,0:T(8,128)S(1)}, u32[]{:S(2)}, u32[]{:S(2)}) collective-permute-start(f32[16,16,128]{2,1,0:T(8,128)S(1)} %all_to_all.10.mine_ref), channel_id=1, source_target_pairs={{0,8},{8,0},{16,24},{24,16},{32,40},{40,32},{48,56},{56,48},{64,72... | collective-permute-start | bytes 393224 | tf_op jit(solution)/shard_map/ppermute | solution.py:343
